TPU v7x, 512 devices: a 8x2x16 block of a 8x8x16 slice. The times are simulated.
512 devices in a mesh: prompt: 2 (over y), seq: 16 (over z), blk: 8 (over x), cfg: 2 (over core).
Axes of the slice: x: 8, y: 2, z: 16, core: 2. Of those that a mesh axis runs over, the one named last changes fastest.
The devices are a block of a 8x8x16 slice.
Arguments:
- queries: bfloat16 [2, 12288, 4096], P('cfg', ('prompt', 'blk', 'seq')), parts along dimension 1, may hold values from -5 to 5
- key_states: bfloat16 [2, 12288, 4096], P('cfg', ('prompt', 'blk', 'seq')), parts along dimension 1, may hold values from -5 to 5
- value_states: bfloat16 [2, 12288, 4096], P('cfg', ('prompt', 'blk', 'seq')), parts along dimension 1, may hold values from -6 to 6
- noisy_latents: float32 [12288, 64], P(('prompt', 'blk', 'seq')), parts along dimension 0, may hold values from -6 to 6
- patch_order: int32 [12288], P(('prompt', 'blk', 'seq')), parts along dimension 0, may hold values from 0 to 6143, as said below
- head_weight: bfloat16 [4096, 64], replicated, may hold values from -0.75 to 0.75
- latent_std: float32 [16], replicated, may hold values from 0.1 to 1.9
- latent_mean: float32 [16], replicated, may hold values from -3 to 3
- conv_weight: bfloat16 [3, 3, 3, 16, 384], replicated, may hold values from -0.3125 to 0.3125
- conv_bias: float32 [384], replicated, may hold values from -2 to 2
Outputs:
- features: bfloat16 [16, 64, 48, 384], P(('prompt', 'cfg'), 'seq', 'blk'), parts along dimension 0
There are 2 independent parts, one for each index of `prompt`. A program takes and returns all parts, laid end to end along the dimension named above; an argument that names none is the same for every part. Nothing has to cross between parts.
Inputs may be any that keep to these rules, and one draw needn't show every extreme that they name: A permutation of 0 to 6143 that keeps every aligned block of 48 tokens within itself: patch_order[t] // 48 == t // 48.
All inputs are finite; a program needn't handle non-finite values.
Results may differ from a plain program's by a relative error of at most 0.012.
Values may be sent and summed in bfloat16 or wider, within the bound.
A program may use at most 128 MiB of HBM per device.

v0:
```python
import math

import jax
import jax.numpy as jnp
from jax import lax
from jax.sharding import PartitionSpec as P

HDIM = 128
ZCH = 16
COLS_DEV = 3


GUIDE = 5.0
NOISE_LEVEL = 0.5


def split_up(array, dim, devices):
    lengths = array.shape
    pieces = array.reshape(*lengths[:dim], devices, lengths[dim] // devices, *lengths[dim + 1 :])
    return jnp.moveaxis(pieces, dim, 0)


def sum_at_owner(array, axis, dim):
    devices = lax.axis_size(axis)
    pieces = lax.all_to_all(split_up(array, dim, devices), axis, 0, 0, tiled=True)
    return jnp.sum(pieces.astype(jnp.float32), axis=0)


def partner(array, axis, apart):
    return lax.ppermute(array, axis, [(i, i ^ 1 << apart) for i in range(lax.axis_size(axis))])


def padded(array, sides, width):
    for axis, dim in sides:
        devices, length = (lax.axis_size(axis), array.shape[dim])
        up = [(i, (i + 1) % devices) for i in range(devices - 1)]
        down = [(j, i) for i, j in up]
        last = lax.slice_in_dim(array, length - width, length, axis=dim)
        first = lax.slice_in_dim(array, 0, width, axis=dim)
        before = lax.ppermute(last, axis, up)
        after = lax.ppermute(first, axis, down)
        array = jnp.concatenate([before, array, after], axis=dim)
    return array


def fold_keys(carry, piece, grouped, block):
    keys_piece, values_piece = piece
    heads = grouped.shape[1]
    count = keys_piece.shape[0] // block
    key_blocks = keys_piece.reshape(count, block, heads, HDIM)
    value_blocks = values_piece.reshape(count, block, heads, HDIM)
    scale = 1.0 / math.sqrt(HDIM)

    def one_block(state, pair):
        top, total, acc = state
        key_block, value_block = pair
        scores = (
            jnp.einsum("qhd,khd->hqk", grouped, key_block, preferred_element_type=jnp.float32)
            * scale
        )
        new_top = jnp.maximum(top, jnp.max(scores, axis=2))
        expo = jnp.exp(scores - new_top[:, :, None])
        factor = jnp.exp(top - new_top)
        total = total * factor + jnp.sum(expo, axis=2)
        weights = expo.astype(jnp.bfloat16)
        update = jnp.einsum(
            "hqk,khd->qhd", weights, value_block, preferred_element_type=jnp.float32
        )
        acc = acc * factor.T[:, :, None] + update
        return ((new_top, total, acc), None)

    state, unused = lax.scan(one_block, carry, (key_blocks, value_blocks))
    return state


def start_for(rows, heads):
    return (
        jnp.full((heads, rows), -1e30, jnp.float32),
        jnp.zeros((heads, rows), jnp.float32),
        jnp.zeros((rows, heads, HDIM), jnp.float32),
    )


def finish(state):
    top, total, acc = state
    rows = acc.shape[0]
    return (acc / total.T[:, :, None]).astype(jnp.bfloat16).reshape(rows, acc.shape[1] * HDIM)


def local(
    queries,
    key_states,
    value_states,
    noisy_latents,
    patch_order,
    head_weight,
    latent_std,
    latent_mean,
    conv_weight,
    conv_bias,
):
    seq_count = lax.axis_size("seq")
    blk_count = lax.axis_size("blk")
    seq_index = lax.axis_index("seq")
    blk_index = lax.axis_index("blk")
    cfg_index = lax.axis_index("cfg")
    tok_rows = queries.shape[1]
    own_query = queries[0]
    own_keys = key_states[0]
    own_values = value_states[0]
    local_query, local_keys, local_values = (
        lax.all_to_all(own_query, "seq", split_axis=1, concat_axis=0, tiled=True),
        lax.all_to_all(own_keys, "seq", split_axis=1, concat_axis=0, tiled=True),
        lax.all_to_all(own_values, "seq", split_axis=1, concat_axis=0, tiled=True),
    )
    frame_rows = local_query.shape[0]
    heads = local_query.shape[1] // HDIM
    grouped = local_query.reshape(frame_rows, heads, HDIM)
    state = fold_keys(
        start_for(frame_rows, heads),
        (
            lax.all_gather(local_keys, "blk", axis=0, tiled=True),
            lax.all_gather(local_values, "blk", axis=0, tiled=True),
        ),
        grouped,
        frame_rows,
    )
    attended = finish(state)
    weight_rows = lax.dynamic_slice_in_dim(
        head_weight, seq_index * attended.shape[1], attended.shape[1], 0
    )
    velocity = sum_at_owner(
        jnp.dot(attended, weight_rows, preferred_element_type=jnp.float32).astype(jnp.bfloat16),
        "seq",
        0,
    )
    other = partner(velocity, "cfg", 0)
    is_cond = cfg_index == 0
    cond = jnp.where(is_cond, velocity, other)
    uncond = jnp.where(is_cond, other, velocity)
    guided = uncond + GUIDE * (cond - uncond)
    denoised = noisy_latents - NOISE_LEVEL * guided
    pixels = (
        denoised * jnp.tile(latent_std, 4)[None, :] + jnp.tile(latent_mean, 4)[None, :]
    ).astype(jnp.bfloat16)
    block_start = (blk_index * seq_count + seq_index) * tok_rows
    local_slot = patch_order - block_start
    selector = (jnp.arange(tok_rows, dtype=jnp.int32)[:, None] == local_slot[None, :]).astype(
        jnp.bfloat16
    )
    placed = jnp.dot(selector, pixels, preferred_element_type=jnp.float32).astype(jnp.bfloat16)
    grid_cols = COLS_DEV * blk_count
    strip_rows = tok_rows // grid_cols
    strip = placed.reshape(1, strip_rows, grid_cols * placed.shape[1])
    received = lax.all_to_all(strip, "blk", split_axis=2, concat_axis=0, tiled=True)
    frame_count = received.shape[0]
    tile = (
        received.reshape(frame_count, strip_rows, COLS_DEV, 2, 2, ZCH)
        .transpose(0, 1, 3, 2, 4, 5)
        .reshape(frame_count, 2 * strip_rows, 2 * COLS_DEV, ZCH)
    )
    half = frame_count // 2
    leading = jnp.zeros((2,) + tile.shape[1:], jnp.bfloat16)
    timeline = jnp.concatenate([leading, tile], axis=0)
    window = lax.dynamic_slice_in_dim(timeline, cfg_index * half, half + 2, 0)
    framed = padded(window, (("seq", 1), ("blk", 2)), 1)
    tile_rows = 2 * strip_rows
    tile_cols = 2 * COLS_DEV
    columns = []
    for step_t in range(3):
        for step_y in range(3):
            for step_x in range(3):
                columns.append(
                    framed[
                        step_t : step_t + half,
                        step_y : step_y + tile_rows,
                        step_x : step_x + tile_cols,
                        :,
                    ]
                )
    stacked = jnp.concatenate(columns, axis=3).reshape(half * tile_rows * tile_cols, 27 * ZCH)
    kernel = conv_weight.reshape(27 * ZCH, conv_weight.shape[4])
    output = jnp.dot(stacked, kernel, preferred_element_type=jnp.float32) + conv_bias[None, :]
    return output.reshape(half, tile_rows, tile_cols, conv_weight.shape[4]).astype(jnp.bfloat16)


def solution(mesh):
    in_specs = (
        P("cfg", ("prompt", "blk", "seq"), None),
        P("cfg", ("prompt", "blk", "seq"), None),
        P("cfg", ("prompt", "blk", "seq"), None),
        P(("prompt", "blk", "seq"), None),
        P(("prompt", "blk", "seq")),
        P(),
        P(),
        P(),
        P(),
        P(),
    )
    out_specs = P(("prompt", "cfg"), "seq", "blk", None)
    return jax.shard_map(local, mesh=mesh, in_specs=in_specs, out_specs=out_specs, check_vma=False)
```

profile of v0, /device:TPU:65, one launch (start us, length us, event | category | flops | bytes accessed | tf_op | source)
XLA Modules:
  0.0 336.8 jit_solution(12205130973058300356)
XLA Ops:
  7.8 62.0 %all_to_all.74 = bf16[48,16,256]{2,0,1:T(8,128)(2,1)} all-to-all(bf16[48,16,256]{2,0,1:T(8,128)(2,1)S(1)} %copy.52), channel_id=1, replica_groups=mesh['prompt'=2,'seq'=16,'blk'=8,'cfg'=2] {'seq'}, dimensions={1} | all-to-all | bytes 786432 | tf_op jit(solution)/shard_map/all_to_all | solution.py:113
  71.2 29.6 %all_to_all.75 = bf16[48,16,256]{2,0,1:T(8,128)(2,1)} all-to-all(bf16[48,16,256]{2,0,1:T(8,128)(2,1)S(1)} %copy.55), channel_id=1, replica_groups=mesh['prompt'=2,'seq'=16,'blk'=8,'cfg'=2] {'seq'}, dimensions={1} | all-to-all | bytes 786432 | tf_op jit(solution)/shard_map/all_to_all | solution.py:114
  101.8 11.6 %all-to-all-start.1 = ((bf16[48,16,256]{2,0,1:T(8,128)(2,1)}), bf16[48,16,256]{2,0,1:T(8,128)(2,1)S(1)}, u32[]{:S(2)}, u32[]{:S(2)}) async-start(bf16[48,16,256]{2,0,1:T(8,128)(2,1)} %copy.54), calls=%async_computation.1 | async-start | bytes 786432 | tf_op jit(solution)/shard_map/all_to_all | solution.py:112
  113.4 17.9 %all-to-all-done.1 = bf16[48,16,256]{2,0,1:T(8,128)(2,1)S(1)} async-done(((bf16[48,16,256]{2,0,1:T(8,128)(2,1)}), bf16[48,16,256]{2,0,1:T(8,128)(2,1)S(1)}, u32[]{:S(2)}, u32[]{:S(2)}) %all-to-all-start.1) | async-done | bytes 393248 | tf_op jit(solution)/shard_map/all_to_all | solution.py:112
  131.5 5.5 %reshape.65 = bf16[8,768,2,128]{3,2,1,0:T(2,128)(2,1)} reshape(bf16[6144,256]{1,0:T(8,128)(2,1)} %all-gather.3.cloned.1.call-done) | data formatting | bytes 6291456 | tf_op jit(solution)/shard_map/reshape | solution.py:50
  137.0 38.1 %all-gather.5.cloned.1.call-done = bf16[6144,256]{1,0:T(8,128)(2,1)} async-done(((bf16[768,256]{1,0:T(8,128)(2,1)}), bf16[6144,256]{1,0:T(8,128)(2,1)}) %all-gather.5.cloned.1.call-update) | async-done | bytes 3145744 | tf_op jit(solution)/shard_map/all_gather | solution.py:123
  175.1 5.5 %reshape.66 = bf16[8,768,2,128]{3,2,1,0:T(2,128)(2,1)} reshape(bf16[6144,256]{1,0:T(8,128)(2,1)} %all-gather.5.cloned.1.call-done) | data formatting | bytes 6291456 | tf_op jit(solution)/shard_map/reshape | solution.py:51
  180.6 77.1 %while.15 = (s32[]{:T(128)}, f32[2,768]{1,0:T(2,128)S(1)}, f32[2,768]{1,0:T(2,128)S(1)}, f32[768,2,128]{0,2,1:T(8,128)S(1)}, bf16[8,768,2,128]{3,2,1,0:T(2,128)(...) while((s32[]{:T(128)}, f32[2,768]{1,0:T(2,128)S(1)}, ...), condition=%wide.region_3.4_spmd.clone, body=%wide.region_0.3_spmd.clone.sunk | while | flops 614016000 | bytes 38240392 | solution.py:72
  185.7 3.6 %fusion.54 = f32[768,2,128]{0,2,1:T(8,128)S(1)} fusion(f32[2,768,768]{2,1,0:T(8,128)} %get-tuple-element.214, f32[2,768]{1,0:T(2,128)S(1)} %get-tuple-element.236, f32[768,2,128]{0,2,1:T(8,128)S(1)} %get-tuple-element.229, bf16[1,768,2,128]{1,3,2,0:T(8,128)(2,1)S(1)} %copy.87, f32[768,2]{0,1:T(2,128)S(1)} %get-tuple-element.216, pred[]{:T(512)S(6)} %compare.4), kind=kOutput, calls=%fused_computation.9.clone.1 | convolution fusion | flops 306118656 | bytes 6696961 | tf_op jit(solution)/shard_map/while/body/eval_jaxpr/hqk,khd->qhd/dot_general | solution.py:66
  195.4 3.6 %fusion.54 = f32[768,2,128]{0,2,1:T(8,128)S(1)} fusion(f32[2,768,768]{2,1,0:T(8,128)} %get-tuple-element.214, f32[2,768]{1,0:T(2,128)S(1)} %get-tuple-element.236, f32[768,2,128]{0,2,1:T(8,128)S(1)} %get-tuple-element.229, bf16[1,768,2,128]{1,3,2,0:T(8,128)(2,1)S(1)} %copy.87, f32[768,2]{0,1:T(2,128)S(1)} %get-tuple-element.216, pred[]{:T(512)S(6)} %compare.4), kind=kOutput, calls=%fused_computation.9.clone.1 | convolution fusion | flops 306118656 | bytes 6696961 | tf_op jit(solution)/shard_map/while/body/eval_jaxpr/hqk,khd->qhd/dot_general | solution.py:66
  205.0 3.6 %fusion.54 = f32[768,2,128]{0,2,1:T(8,128)S(1)} fusion(f32[2,768,768]{2,1,0:T(8,128)} %get-tuple-element.214, f32[2,768]{1,0:T(2,128)S(1)} %get-tuple-element.236, f32[768,2,128]{0,2,1:T(8,128)S(1)} %get-tuple-element.229, bf16[1,768,2,128]{1,3,2,0:T(8,128)(2,1)S(1)} %copy.87, f32[768,2]{0,1:T(2,128)S(1)} %get-tuple-element.216, pred[]{:T(512)S(6)} %compare.4), kind=kOutput, calls=%fused_computation.9.clone.1 | convolution fusion | flops 306118656 | bytes 6696961 | tf_op jit(solution)/shard_map/while/body/eval_jaxpr/hqk,khd->qhd/dot_general | solution.py:66
  214.6 3.6 %fusion.54 = f32[768,2,128]{0,2,1:T(8,128)S(1)} fusion(f32[2,768,768]{2,1,0:T(8,128)} %get-tuple-element.214, f32[2,768]{1,0:T(2,128)S(1)} %get-tuple-element.236, f32[768,2,128]{0,2,1:T(8,128)S(1)} %get-tuple-element.229, bf16[1,768,2,128]{1,3,2,0:T(8,128)(2,1)S(1)} %copy.87, f32[768,2]{0,1:T(2,128)S(1)} %get-tuple-element.216, pred[]{:T(512)S(6)} %compare.4), kind=kOutput, calls=%fused_computation.9.clone.1 | convolution fusion | flops 306118656 | bytes 6696961 | tf_op jit(solution)/shard_map/while/body/eval_jaxpr/hqk,khd->qhd/dot_general | solution.py:66
  224.3 3.6 %fusion.54 = f32[768,2,128]{0,2,1:T(8,128)S(1)} fusion(f32[2,768,768]{2,1,0:T(8,128)} %get-tuple-element.214, f32[2,768]{1,0:T(2,128)S(1)} %get-tuple-element.236, f32[768,2,128]{0,2,1:T(8,128)S(1)} %get-tuple-element.229, bf16[1,768,2,128]{1,3,2,0:T(8,128)(2,1)S(1)} %copy.87, f32[768,2]{0,1:T(2,128)S(1)} %get-tuple-element.216, pred[]{:T(512)S(6)} %compare.4), kind=kOutput, calls=%fused_computation.9.clone.1 | convolution fusion | flops 306118656 | bytes 6696961 | tf_op jit(solution)/shard_map/while/body/eval_jaxpr/hqk,khd->qhd/dot_general | solution.py:66
  233.9 3.6 %fusion.54 = f32[768,2,128]{0,2,1:T(8,128)S(1)} fusion(f32[2,768,768]{2,1,0:T(8,128)} %get-tuple-element.214, f32[2,768]{1,0:T(2,128)S(1)} %get-tuple-element.236, f32[768,2,128]{0,2,1:T(8,128)S(1)} %get-tuple-element.229, bf16[1,768,2,128]{1,3,2,0:T(8,128)(2,1)S(1)} %copy.87, f32[768,2]{0,1:T(2,128)S(1)} %get-tuple-element.216, pred[]{:T(512)S(6)} %compare.4), kind=kOutput, calls=%fused_computation.9.clone.1 | convolution fusion | flops 306118656 | bytes 6696961 | tf_op jit(solution)/shard_map/while/body/eval_jaxpr/hqk,khd->qhd/dot_general | solution.py:66
  243.5 3.6 %fusion.54 = f32[768,2,128]{0,2,1:T(8,128)S(1)} fusion(f32[2,768,768]{2,1,0:T(8,128)} %get-tuple-element.214, f32[2,768]{1,0:T(2,128)S(1)} %get-tuple-element.236, f32[768,2,128]{0,2,1:T(8,128)S(1)} %get-tuple-element.229, bf16[1,768,2,128]{1,3,2,0:T(8,128)(2,1)S(1)} %copy.87, f32[768,2]{0,1:T(2,128)S(1)} %get-tuple-element.216, pred[]{:T(512)S(6)} %compare.4), kind=kOutput, calls=%fused_computation.9.clone.1 | convolution fusion | flops 306118656 | bytes 6696961 | tf_op jit(solution)/shard_map/while/body/eval_jaxpr/hqk,khd->qhd/dot_general | solution.py:66
  253.2 3.6 %fusion.54 = f32[768,2,128]{0,2,1:T(8,128)S(1)} fusion(f32[2,768,768]{2,1,0:T(8,128)} %get-tuple-element.214, f32[2,768]{1,0:T(2,128)S(1)} %get-tuple-element.236, f32[768,2,128]{0,2,1:T(8,128)S(1)} %get-tuple-element.229, bf16[1,768,2,128]{1,3,2,0:T(8,128)(2,1)S(1)} %copy.87, f32[768,2]{0,1:T(2,128)S(1)} %get-tuple-element.216, pred[]{:T(512)S(6)} %compare.4), kind=kOutput, calls=%fused_computation.9.clone.1 | convolution fusion | flops 306118656 | bytes 6696961 | tf_op jit(solution)/shard_map/while/body/eval_jaxpr/hqk,khd->qhd/dot_general | solution.py:66
  259.1 12.8 %all-to-all-start.3 = ((bf16[16,2,1536]{2,1,0:T(2,128)(2,1)}), bf16[16,2,1536]{2,1,0:T(2,128)(2,1)S(1)}, u32[]{:S(2)}, u32[]{:S(2)}) async-start(bf16[16,2,1536]{2,1,0:T(2,128)(2,1)} %reshape.67), calls=%async_computation.3 | async-start | bytes 196608 | tf_op jit(solution)/shard_map/all_to_all | solution.py:25
  271.9 11.6 %all-to-all-done.3 = bf16[16,2,1536]{2,1,0:T(2,128)(2,1)S(1)} async-done(((bf16[16,2,1536]{2,1,0:T(2,128)(2,1)}), bf16[16,2,1536]{2,1,0:T(2,128)(2,1)S(1)}, u32[]{:S(2)}, u32[]{:S(2)}) %all-to-all-start.3) | async-done | bytes 98336 | tf_op jit(solution)/shard_map/all_to_all | solution.py:25
  283.8 5.5 %collective-permute-start = (f32[48,64]{0,1:T(8,128)S(1)}, f32[48,64]{0,1:T(8,128)S(1)}, u32[]{:S(2)}, u32[]{:S(2)}) collective-permute-start(f32[48,64]{0,1:T(8,128)S(1)} %copy.76), channel_id=1, source_target_pairs={{0,1},{1,0},{2,3},{3,2},{4,5},{5,4},{6,7},{7,6},{8,9},{9,8},{10,11... | collective-permute-start | bytes 36872 | tf_op jit(solution)/shard_map/ppermute | solution.py:30
  291.4 8.8 %reduce = bf16[1536,2]{1,0:T(8,128)(2,1)S(1)} reduce(bf16[1536,1,2]{2,1,0:T(2,128)(2,1)S(1)} %bitcast.77, bf16[]{:T(256)} %broadcast.58), dimensions={1}, to_apply=%bitcast.53.reduce_sub_computation | reduce | bytes 12290
  301.3 4.4 %all-to-all-start.4 = ((bf16[8,2,192]{2,1,0:T(2,128)(2,1)}), bf16[8,2,192]{2,1,0:T(2,128)(2,1)S(1)}, u32[]{:S(2)}, u32[]{:S(2)}) async-start(bf16[8,2,192]{2,1,0:T(2,128)(2,1)} %reshape.69), calls=%async_computation.4 | async-start | bytes 16384 | tf_op jit(solution)/shard_map/all_to_all | solution.py:155
  305.7 6.6 %all-to-all-done.4 = bf16[8,2,192]{2,1,0:T(2,128)(2,1)S(1)} async-done(((bf16[8,2,192]{2,1,0:T(2,128)(2,1)}), bf16[8,2,192]{2,1,0:T(2,128)(2,1)S(1)}, u32[]{:S(2)}, u32[]{:S(2)}) %all-to-all-start.4) | async-done | bytes 6176 | tf_op jit(solution)/shard_map/all_to_all | solution.py:155
  318.1 3.0 collective-permute-done.2
  324.7 3.1 collective-permute-done.4
  (147 shorter events, 67.6 us)
Async XLA Ops:
  6.5 251.3 %copy-start = (bf16[4096,64]{0,1:T(8,128)(2,1)S(1)}, bf16[4096,64]{0,1:T(8,128)(2,1)}, u32[]{:S(2)}) copy-start(bf16[4096,64]{0,1:T(8,128)(2,1)} %param.17) | copy-start | bytes 1572868
  6.6 94.3 %copy-start.2 = (bf16[1,48,4096]{2,1,0:T(8,128)(2,1)S(1)}, bf16[1,48,4096]{2,1,0:T(8,128)(2,1)}, u32[]{:S(2)}) copy-start(bf16[1,48,4096]{2,1,0:T(8,128)(2,1)} %param.12) | copy-start | bytes 1179652
  6.6 124.9 %all-gather.3.cloned.1.call-start = ((), (), s32[]{:S(2)}) async-start(), calls=%async_computation.5 | async-start | bytes 3538944 | tf_op jit(solution)/shard_map/all_gather | solution.py:122
  69.9 105.2 %all-gather.5.cloned.1.call-start = ((), (), s32[]{:S(2)}) async-start(), calls=%async_computation.6 | async-start | bytes 3538944 | tf_op jit(solution)/shard_map/all_gather | solution.py:123
  101.8 29.5 %all-to-all-start.1 = ((bf16[48,16,256]{2,0,1:T(8,128)(2,1)}), bf16[48,16,256]{2,0,1:T(8,128)(2,1)S(1)}, u32[]{:S(2)}, u32[]{:S(2)}) async-start(bf16[48,16,256]{2,0,1:T(8,128)(2,1)} %copy.54), calls=%async_computation.1 | async-start | bytes 786432 | tf_op jit(solution)/shard_map/all_to_all | solution.py:112
  180.6 108.7 %copy-start.8 = (s32[48]{0:T(128)S(1)}, s32[48]{0:T(128)}, u32[]{:S(2)}) copy-start(s32[48]{0:T(128)} %param.16) | copy-start | bytes 580
  180.6 108.7 %copy-start.4 = (f32[48,64]{1,0:T(8,128)S(1)}, f32[48,64]{1,0:T(8,128)}, u32[]{:S(2)}) copy-start(f32[48,64]{1,0:T(8,128)} %param.15) | copy-start | bytes 36868
  180.6 108.8 %copy-start.6 = (f32[16]{0:T(128)S(1)}, f32[16]{0:T(128)}, u32[]{:S(2)}) copy-start(f32[16]{0:T(128)} %param.19) | copy-start | bytes 196
  180.6 108.9 %copy-start.7 = (f32[16]{0:T(128)S(1)}, f32[16]{0:T(128)}, u32[]{:S(2)}) copy-start(f32[16]{0:T(128)} %param.18) | copy-start | bytes 196
  185.7 3.8 %copy-start.1 = (f32[2,768,768]{2,1,0:T(8,128)S(1)}, f32[2,768,768]{2,1,0:T(8,128)}, u32[]{:S(2)}) copy-start(f32[2,768,768]{2,1,0:T(8,128)} %get-tuple-element.214) | copy-start | bytes 14155780 | tf_op jit(solution)/shard_map/while
  195.4 3.8 %copy-start.1 = (f32[2,768,768]{2,1,0:T(8,128)S(1)}, f32[2,768,768]{2,1,0:T(8,128)}, u32[]{:S(2)}) copy-start(f32[2,768,768]{2,1,0:T(8,128)} %get-tuple-element.214) | copy-start | bytes 14155780 | tf_op jit(solution)/shard_map/while
  205.0 3.8 %copy-start.1 = (f32[2,768,768]{2,1,0:T(8,128)S(1)}, f32[2,768,768]{2,1,0:T(8,128)}, u32[]{:S(2)}) copy-start(f32[2,768,768]{2,1,0:T(8,128)} %get-tuple-element.214) | copy-start | bytes 14155780 | tf_op jit(solution)/shard_map/while
  214.6 3.8 %copy-start.1 = (f32[2,768,768]{2,1,0:T(8,128)S(1)}, f32[2,768,768]{2,1,0:T(8,128)}, u32[]{:S(2)}) copy-start(f32[2,768,768]{2,1,0:T(8,128)} %get-tuple-element.214) | copy-start | bytes 14155780 | tf_op jit(solution)/shard_map/while
  224.3 3.8 %copy-start.1 = (f32[2,768,768]{2,1,0:T(8,128)S(1)}, f32[2,768,768]{2,1,0:T(8,128)}, u32[]{:S(2)}) copy-start(f32[2,768,768]{2,1,0:T(8,128)} %get-tuple-element.214) | copy-start | bytes 14155780 | tf_op jit(solution)/shard_map/while
  233.9 3.8 %copy-start.1 = (f32[2,768,768]{2,1,0:T(8,128)S(1)}, f32[2,768,768]{2,1,0:T(8,128)}, u32[]{:S(2)}) copy-start(f32[2,768,768]{2,1,0:T(8,128)} %get-tuple-element.214) | copy-start | bytes 14155780 | tf_op jit(solution)/shard_map/while
  257.8 71.2 %copy-start.3 = (bf16[3,3,3,16,384]{4,3,2,1,0:T(8,128)(2,1)S(1)}, bf16[3,3,3,16,384]{4,3,2,1,0:T(8,128)(2,1)}, u32[]{:S(2)}) copy-start(bf16[3,3,3,16,384]{4,3,2,1,0:T(8,128)(2,1)} %param.20) | copy-start | bytes 995332
  257.8 71.2 %copy-start.5 = (f32[384]{0:T(512)S(1)}, f32[384]{0:T(512)}, u32[]{:S(2)}) copy-start(f32[384]{0:T(512)} %param.21) | copy-start | bytes 4612
  259.1 24.5 %all-to-all-start.3 = ((bf16[16,2,1536]{2,1,0:T(2,128)(2,1)}), bf16[16,2,1536]{2,1,0:T(2,128)(2,1)S(1)}, u32[]{:S(2)}, u32[]{:S(2)}) async-start(bf16[16,2,1536]{2,1,0:T(2,128)(2,1)} %reshape.67), calls=%async_computation.3 | async-start | bytes 196608 | tf_op jit(solution)/shard_map/all_to_all | solution.py:25
  283.8 6.1 %collective-permute-start = (f32[48,64]{0,1:T(8,128)S(1)}, f32[48,64]{0,1:T(8,128)S(1)}, u32[]{:S(2)}, u32[]{:S(2)}) collective-permute-start(f32[48,64]{0,1:T(8,128)S(1)} %copy.76), channel_id=1, source_target_pairs={{0,1},{1,0},{2,3},{3,2},{4,5},{5,4},{6,7},{7,6},{8,9},{9,8},{10,11... | collective-permute-start | bytes 36872 | tf_op jit(solution)/shard_map/ppermute | solution.py:30
  301.3 10.9 %all-to-all-start.4 = ((bf16[8,2,192]{2,1,0:T(2,128)(2,1)}), bf16[8,2,192]{2,1,0:T(2,128)(2,1)S(1)}, u32[]{:S(2)}, u32[]{:S(2)}) async-start(bf16[8,2,192]{2,1,0:T(2,128)(2,1)} %reshape.69), calls=%async_computation.4 | async-start | bytes 16384 | tf_op jit(solution)/shard_map/all_to_all | solution.py:155
  314.0 4.1 %collective-permute-start.1 = (bf16[6,1,6,16]{3,0,2,1:T(8,128)(2,1)S(1)}, bf16[6,1,6,16]{3,0,2,1:T(8,128)(2,1)S(1)}, u32[]{:S(2)}, u32[]{:S(2)}) collective-permute-start(bf16[6,1,6,16]{3,0,2,1:T(8,128)(2,1)S(1)} %get-tuple-element.151), channel_id=1, source_target_pairs={{0,16},{16,32},{32,48},{48,64},{64,80},{80,96},{96,112},{112,128},... | collective-permute-start | bytes 3464 | tf_op jit(solution)/shard_map/ppermute | solution.py:40
  316.6 4.5 %collective-permute-start.2 = (bf16[6,1,6,16]{3,0,2,1:T(8,128)(2,1)S(1)}, bf16[6,1,6,16]{3,0,2,1:T(8,128)(2,1)S(1)}, u32[]{:S(2)}, u32[]{:S(2)}) collective-permute-start(bf16[6,1,6,16]{3,0,2,1:T(8,128)(2,1)S(1)} %get-tuple-element.152), channel_id=1, source_target_pairs={{16,0},{32,16},{48,32},{64,48},{80,64},{96,80},{112,96},{128,112},... | collective-permute-start | bytes 3464 | tf_op jit(solution)/shard_map/ppermute | solution.py:41
  321.1 3.6 %collective-permute-start.3 = (bf16[6,6,1,16]{3,0,2,1:T(8,128)(2,1)S(1)}, bf16[6,6,1,16]{3,0,2,1:T(8,128)(2,1)S(1)}, u32[]{:S(2)}, u32[]{:S(2)}) collective-permute-start(bf16[6,6,1,16]{3,0,2,1:T(8,128)(2,1)S(1)} %get-tuple-element.138), channel_id=1, source_target_pairs={{0,2},{2,4},{4,6},{6,8},{8,10},{10,12},{12,14},{1,3},{3,5},{5,7},{... | collective-permute-start | bytes 3464 | tf_op jit(solution)/shard_map/ppermute | solution.py:40
  323.3 4.5 %collective-permute-start.4 = (bf16[6,6,1,16]{3,0,2,1:T(8,128)(2,1)S(1)}, bf16[6,6,1,16]{3,0,2,1:T(8,128)(2,1)S(1)}, u32[]{:S(2)}, u32[]{:S(2)}) collective-permute-start(bf16[6,6,1,16]{3,0,2,1:T(8,128)(2,1)S(1)} %get-tuple-element.137), channel_id=1, source_target_pairs={{2,0},{4,2},{6,4},{8,6},{10,8},{12,10},{14,12},{3,1},{5,3},{7,5},{... | collective-permute-start | bytes 3464 | tf_op jit(solution)/shard_map/ppermute | solution.py:41
  (2 other events, 7.5 us)
Sparse Core Ops, SparseCore 0:
  70.0 52.5 all-gather.2
  124.7 50.3 all-gather.4
where the time goes:
time: 340 us; the launch traced here: 337 us
  blocking collectives  91.6 us (27%)
  waiting for transfers between devices  80.7 us (24%)
  matrix products  53 us (16%)
  starting transfers between devices  41.8 us (12%)
  local copies, waits for them, and re-layouts  39.8 us (12%)
  other arithmetic  15.6 us (5%)
  between operations  13.8 us (4%)
    all_to_all x1, blocking collectives, local(): lax.all_to_all(own_keys, 'seq', split_axis=1, concat_axis=0, tiled=True)  62 us
    all_gather x1, waiting for transfers between devices, local(): lax.all_gather(local_values, 'blk', axis=0, tiled=True)  38.1 us
    all_to_all x1, blocking collectives, local(): lax.all_to_all(own_values, 'seq', split_axis=1, concat_axis=0, tiled=True)  29.6 us
    dot_general x8, matrix products, one_block(): jnp.einsum('hqk,khd->qhd', weights, value_block, preferred_element_type=j...  29.1 us
    dot_general x8, matrix products, one_block(): jnp.einsum('qhd,khd->hqk', grouped, key_block, preferred_element_type=jnp...  23.3 us
    all_to_all x1, waiting for transfers between devices, local(): lax.all_to_all(own_query, 'seq', split_axis=1, concat_axis=0, tiled=True)  17.9 us
    dynamic_slice x16, local copies, waits for them, and re-layouts, fold_keys(): state, unused = lax.scan(one_block, carry, (key_blocks, value_blocks))  16.8 us
    all_to_all x1, starting transfers between devices, sum_at_owner(): lax.all_to_all(split_up(array, dim, devices), axis, 0, 0, tiled=True)  12.8 us
  transfers between devices with their start and end apart: 10, of which 7 were waited for; matrix products, arithmetic and copies ran while one was open for 2% of the time, Pallas kernels for 0%

commit v1 on v0

--- a/solution.py
+++ b/solution.py
@@ -1,17 +1,232 @@
+import functools
 import math
 
 import jax
 import jax.numpy as jnp
 from jax import lax
+from jax.experimental import pallas as pl
+from jax.experimental.pallas import tpu as pltpu
 from jax.sharding import PartitionSpec as P
 
 HDIM = 128
 ZCH = 16
 COLS_DEV = 3
-
-
 GUIDE = 5.0
 NOISE_LEVEL = 0.5
+MESH = pl.DeviceIdType.MESH
+EXP_SCALE = math.log2(math.e) / math.sqrt(HDIM)
+
+
+def exchange_kernel(
+    nz, nx, q_ref, k_ref, v_ref, w_ref, out_ref,
+    vsend, gx, qx, vt, top, total, acc, zsend, zrecv, xsend, xrecv,
+):
+    seq = lax.axis_index("seq")
+    blk = lax.axis_index("blk")
+    tok = q_ref.shape[0]
+    rows = gx.shape[2]
+    part = rows // 2
+    patch = w_ref.shape[1]
+    hops = nx // 2
+    right = lax.rem(blk + 1, nx)
+    left = lax.rem(blk + nx - 1, nx)
+
+    barrier = pltpu.get_barrier_semaphore()
+
+    def greet(d, _):
+        pl.semaphore_signal(
+            barrier, inc=1, device_id={"seq": lax.rem(seq + d, nz)}, device_id_type=MESH
+        )
+        return 0
+
+    lax.fori_loop(1, nz, greet, 0)
+    pl.semaphore_signal(barrier, inc=1, device_id={"blk": right}, device_id_type=MESH)
+    pl.semaphore_signal(barrier, inc=1, device_id={"blk": left}, device_id_type=MESH)
+
+    def project(s, _):
+        both = []
+        for h in range(2):
+            at = pl.ds(pl.multiple_of((2 * s + h) * HDIM, HDIM), HDIM)
+            both.append(
+                jnp.dot(v_ref[:, at], w_ref[at, :], preferred_element_type=jnp.float32)
+            )
+        vsend[s] = jnp.concatenate(both, axis=1).astype(jnp.bfloat16)
+        return 0
+
+    lax.fori_loop(0, nz, project, 0)
+    pl.semaphore_wait(barrier, nz + 1)
+
+    own_rows = pl.ds(pl.multiple_of(seq * tok, tok), tok)
+
+    def columns(ref, s, h):
+        return ref.at[:, pl.ds(pl.multiple_of((2 * s + h) * HDIM, HDIM), HDIM)]
+
+    sources = (
+        lambda s: columns(k_ref, s, 0),
+        lambda s: vsend.at[s],
+        lambda s: columns(q_ref, s, 0),
+        lambda s: columns(k_ref, s, 1),
+        lambda s: columns(q_ref, s, 1),
+    )
+    whole = (gx.at[0, blk], gx.at[1, blk], qx.at[0], gx.at[2, blk], qx.at[1])
+
+    def spread(i):
+        pltpu.make_async_copy(
+            sources[i](seq), whole[i].at[own_rows, :], zrecv.at[i]
+        ).start()
+
+        def send(d, _):
+            far = (d + 1) // 2
+            peer = lax.rem(seq + jnp.where(lax.rem(d, 2) == 1, far, nz - far), nz)
+            pltpu.make_async_remote_copy(
+                src_ref=sources[i](peer),
+                dst_ref=whole[i].at[own_rows, :],
+                send_sem=zsend.at[i],
+                recv_sem=zrecv.at[i],
+                device_id={"seq": peer},
+                device_id_type=MESH,
+            ).start()
+            return 0
+
+        lax.fori_loop(1, nz, send, 0)
+
+    def spread_done(i):
+        pltpu.make_async_copy(whole[i], whole[i], zrecv.at[i]).wait()
+
+    def ring(c, way, step, half):
+        block = lax.rem(blk + (nx - step + 1 if way == 0 else step - 1), nx)
+        piece = gx.at[c, block, pl.ds(half * part, part), :]
+        return pltpu.make_async_remote_copy(
+            src_ref=piece,
+            dst_ref=piece,
+            send_sem=xsend.at[c, way, step - 1, half],
+            recv_sem=xrecv.at[c, way, step - 1, half],
+            device_id={"blk": right if way == 0 else left},
+            device_id_type=MESH,
+        )
+
+    def travels(way, step, half):
+        return step < hops or (step == hops and way == half)
+
+    def begin(c):
+        for half in range(2):
+            for way in range(2):
+                if travels(way, 1, half):
+                    ring(c, way, 1, half).start()
+
+    def advance(c, step):
+        for half in range(2):
+            for way in range(2):
+                if travels(way, step, half):
+                    ring(c, way, step, half).wait_recv()
+                    if travels(way, step + 1, half):
+                        ring(c, way, step + 1, half).start()
+
+    qtile = 256
+
+    def attend(h, block):
+        if h == 0:
+            vt[block] = gx[1, block].T
+        keys = gx[2 * h, block]
+        values = vt[block, pl.ds(h * patch, patch), :]
+        for t in range(rows // qtile):
+            at = pl.ds(t * qtile, qtile)
+            scores = lax.dot_general(
+                keys, qx[h, at, :], (((1,), (1,)), ((), ())),
+                preferred_element_type=jnp.float32,
+            )
+            old = top[h, :, at]
+            new = jnp.maximum(old, jnp.max(scores, axis=0, keepdims=True))
+            expo = jnp.exp2(scores * EXP_SCALE - new * EXP_SCALE)
+            factor = jnp.exp2((old - new) * EXP_SCALE)
+            top[h, :, at] = new
+            total[h, :, at] = total[h, :, at] * factor + jnp.sum(expo, axis=0, keepdims=True)
+            acc[h, :, at] = acc[h, :, at] * factor + jnp.dot(
+                values, expo.astype(jnp.bfloat16), preferred_element_type=jnp.float32
+            )
+
+    def near(h, step):
+        def one(way, _):
+            block = lax.rem(blk + jnp.where(way == 0, nx - step, step), nx)
+            attend(h, block)
+            return 0
+
+        lax.fori_loop(0, 2, one, 0)
+
+    for i in range(5):
+        spread(i)
+    top[...] = jnp.full(top.shape, -1e30, jnp.float32)
+    total[...] = jnp.zeros(total.shape, jnp.float32)
+    acc[...] = jnp.zeros(acc.shape, jnp.float32)
+
+    spread_done(0)
+    begin(0)
+    for step in range(1, hops - 1):
+        advance(0, step)
+    spread_done(1)
+    begin(1)
+    for step in range(hops - 1, hops + 1):
+        advance(0, step)
+    spread_done(2)
+    attend(0, blk)
+    for step in range(1, hops):
+        advance(1, step)
+        if step == hops - 1:
+            spread_done(3)
+            begin(2)
+        near(0, step)
+    advance(1, hops)
+    attend(0, lax.rem(blk + hops, nx))
+    spread_done(4)
+    attend(1, blk)
+    for step in range(1, hops):
+        advance(2, step)
+        near(1, step)
+    advance(2, hops)
+    attend(1, lax.rem(blk + hops, nx))
+
+    velocity = acc[0] / total[0] + acc[1] / total[1]
+    wide = jnp.concatenate([velocity, jnp.zeros_like(velocity)], axis=0)
+    out_ref[...] = wide.T.astype(jnp.bfloat16)
+
+    for i in range(5):
+        sent = whole[i].at[pl.ds(0, rows - tok), :]
+        pltpu.make_async_copy(sent, sent, zsend.at[i]).wait()
+    for c in range(3):
+        for step in range(1, hops + 1):
+            for half in range(2):
+                for way in range(2):
+                    if travels(way, step, half):
+                        ring(c, way, step, half).wait_send()
+
+
+def share_of_velocity(queries, key_states, value_states, head_weight):
+    nz = lax.axis_size("seq")
+    nx = lax.axis_size("blk")
+    tok = queries.shape[0]
+    rows = nz * tok
+    patch = head_weight.shape[1]
+    vmem = pl.BlockSpec(memory_space=pltpu.VMEM)
+    return pl.pallas_call(
+        functools.partial(exchange_kernel, nz, nx),
+        out_shape=jax.ShapeDtypeStruct((rows, 2 * patch), jnp.bfloat16),
+        in_specs=[vmem] * 4,
+        out_specs=vmem,
+        scratch_shapes=[
+            pltpu.VMEM((nz, tok, 2 * patch), jnp.bfloat16),
+            pltpu.VMEM((3, nx, rows, HDIM), jnp.bfloat16),
+            pltpu.VMEM((2, rows, HDIM), jnp.bfloat16),
+            pltpu.VMEM((nx, 2 * patch, rows), jnp.bfloat16),
+            pltpu.VMEM((2, 1, rows), jnp.float32),
+            pltpu.VMEM((2, 1, rows), jnp.float32),
+            pltpu.VMEM((2, patch, rows), jnp.float32),
+            pltpu.SemaphoreType.DMA((5,)),
+            pltpu.SemaphoreType.DMA((5,)),
+            pltpu.SemaphoreType.DMA((3, 2, nx // 2, 2)),
+            pltpu.SemaphoreType.DMA((3, 2, nx // 2, 2)),
+        ],
+        compiler_params=pltpu.CompilerParams(collective_id=0, has_side_effects=True),
+    )(queries, key_states, value_states, head_weight)
 
 
 def split_up(array, dim, devices):
@@ -41,50 +256,6 @@
         after = lax.ppermute(first, axis, down)
         array = jnp.concatenate([before, array, after], axis=dim)
     return array
-
-
-def fold_keys(carry, piece, grouped, block):
-    keys_piece, values_piece = piece
-    heads = grouped.shape[1]
-    count = keys_piece.shape[0] // block
-    key_blocks = keys_piece.reshape(count, block, heads, HDIM)
-    value_blocks = values_piece.reshape(count, block, heads, HDIM)
-    scale = 1.0 / math.sqrt(HDIM)
-
-    def one_block(state, pair):
-        top, total, acc = state
-        key_block, value_block = pair
-        scores = (
-            jnp.einsum("qhd,khd->hqk", grouped, key_block, preferred_element_type=jnp.float32)
-            * scale
-        )
-        new_top = jnp.maximum(top, jnp.max(scores, axis=2))
-        expo = jnp.exp(scores - new_top[:, :, None])
-        factor = jnp.exp(top - new_top)
-        total = total * factor + jnp.sum(expo, axis=2)
-        weights = expo.astype(jnp.bfloat16)
-        update = jnp.einsum(
-            "hqk,khd->qhd", weights, value_block, preferred_element_type=jnp.float32
-        )
-        acc = acc * factor.T[:, :, None] + update
-        return ((new_top, total, acc), None)
-
-    state, unused = lax.scan(one_block, carry, (key_blocks, value_blocks))
-    return state
-
-
-def start_for(rows, heads):
-    return (
-        jnp.full((heads, rows), -1e30, jnp.float32),
-        jnp.zeros((heads, rows), jnp.float32),
-        jnp.zeros((rows, heads, HDIM), jnp.float32),
-    )
-
-
-def finish(state):
-    top, total, acc = state
-    rows = acc.shape[0]
-    return (acc / total.T[:, :, None]).astype(jnp.bfloat16).reshape(rows, acc.shape[1] * HDIM)
 
 
 def local(
@@ -105,35 +276,8 @@
     blk_index = lax.axis_index("blk")
     cfg_index = lax.axis_index("cfg")
     tok_rows = queries.shape[1]
-    own_query = queries[0]
-    own_keys = key_states[0]
-    own_values = value_states[0]
-    local_query, local_keys, local_values = (
-        lax.all_to_all(own_query, "seq", split_axis=1, concat_axis=0, tiled=True),
-        lax.all_to_all(own_keys, "seq", split_axis=1, concat_axis=0, tiled=True),
-        lax.all_to_all(own_values, "seq", split_axis=1, concat_axis=0, tiled=True),
-    )
-    frame_rows = local_query.shape[0]
-    heads = local_query.shape[1] // HDIM
-    grouped = local_query.reshape(frame_rows, heads, HDIM)
-    state = fold_keys(
-        start_for(frame_rows, heads),
-        (
-            lax.all_gather(local_keys, "blk", axis=0, tiled=True),
-            lax.all_gather(local_values, "blk", axis=0, tiled=True),
-        ),
-        grouped,
-        frame_rows,
-    )
-    attended = finish(state)
-    weight_rows = lax.dynamic_slice_in_dim(
-        head_weight, seq_index * attended.shape[1], attended.shape[1], 0
-    )
-    velocity = sum_at_owner(
-        jnp.dot(attended, weight_rows, preferred_element_type=jnp.float32).astype(jnp.bfloat16),
-        "seq",
-        0,
-    )
+    share = share_of_velocity(queries[0], key_states[0], value_states[0], head_weight)
+    velocity = sum_at_owner(share[:, : head_weight.shape[1]], "seq", 0)
     other = partner(velocity, "cfg", 0)
     is_cond = cfg_index == 0
     cond = jnp.where(is_cond, velocity, other)

time: 340 us -> 197 us (0.58)
  Pallas kernels: 0 us -> 115 us
  blocking collectives: 91.6 us -> 0 us
  waiting for transfers between devices: 80.7 us -> 24.4 us
  matrix products: 53 us -> 0.34 us
  local copies, waits for them, and re-layouts: 39.8 us -> 12.3 us
  between operations: 13.8 us -> 0.27 us
  starting transfers between devices: 41.8 us -> 32.5 us
  other arithmetic: 15.6 us -> 8.99 us
    pallas_call x0 -> x1, Pallas kernels: none -> 115 us  [share_of_velocity(): pl.pallas_call(functools.partial(exchange_kernel, nz, nx), out_shape=jax....]
    all_to_all x2 -> x0, blocking collectives: 91.6 us -> none  [the longest x1 62 us: local(): lax.all_to_all(own_keys, 'seq', split_axis=1, concat_axis=0, tiled=True)]
    dot_general x17 -> x0, matrix products: 52.6 us -> none  [the longest x8 29.1 us: one_block(): jnp.einsum('hqk,khd->qhd', weights, value_block, preferred_element_type=j...]
    all_gather x2 -> x0, waiting for transfers between devices: 38.1 us -> none  [the longest x1 38.1 us: local(): lax.all_gather(local_values, 'blk', axis=0, tiled=True)]
    all_to_all x1 -> x0, waiting for transfers between devices: 17.9 us -> none  [local(): lax.all_to_all(own_query, 'seq', split_axis=1, concat_axis=0, tiled=True)]
    dynamic_slice x16 -> x0, local copies, waits for them, and re-layouts: 16.8 us -> none  [fold_keys(): state, unused = lax.scan(one_block, carry, (key_blocks, value_blocks))]
    all_to_all x1 -> x0, starting transfers between devices: 11.6 us -> none  [local(): lax.all_to_all(own_query, 'seq', split_axis=1, concat_axis=0, tiled=True)]
    reshape x4 -> x0, local copies, waits for them, and re-layouts: 11.3 us -> none  [the longest x1 5.51 us: fold_keys(): key_blocks = keys_piece.reshape(count, block, heads, HDIM)]
  transfers between devices with their start and end apart: 10 -> 7, of which waited for: 7 -> 4; matrix products, arithmetic and copies ran while one was open for 2% -> 0% of each run, Pallas kernels for 0% -> 0%
where the time goes in v1:
time: 197 us; the launch traced here: 194 us
  Pallas kernels  115 us (58%)
  starting transfers between devices  32.5 us (16%)
  waiting for transfers between devices  24.4 us (12%)
  local copies, waits for them, and re-layouts  12.3 us (6%)
  other arithmetic  8.99 us (5%)
    pallas_call x1, Pallas kernels, share_of_velocity(): pl.pallas_call(functools.partial(exchange_kernel, nz, nx), out_shape=jax....  115 us
    all_to_all x1, waiting for transfers between devices, sum_at_owner(): lax.all_to_all(split_up(array, dim, devices), axis, 0, 0, tiled=True)  11.7 us
    all_to_all x1, starting transfers between devices, sum_at_owner(): lax.all_to_all(split_up(array, dim, devices), axis, 0, 0, tiled=True)  11.7 us
    unnamed x1, other arithmetic  8.81 us
    unnamed x18, local copies, waits for them, and re-layouts  8.7 us
    ppermute x1, starting transfers between devices, partner(): lax.ppermute(array, axis, [(i, i ^ 1 << apart) for i in range(lax.axis_si...  8.39 us
    all_to_all x1, waiting for transfers between devices, local(): lax.all_to_all(strip, 'blk', split_axis=2, concat_axis=0, tiled=True)  6.58 us
    ppermute x2, waiting for transfers between devices, padded(): after = lax.ppermute(first, axis, down)  6.05 us
  transfers between devices with their start and end apart: 7, of which 4 were waited for; matrix products, arithmetic and copies ran while one was open for 0% of the time, Pallas kernels for 0%

profile of v1, /device:TPU:65, one launch (start us, length us, event | category | flops | bytes accessed | tf_op | source)
XLA Modules:
  0.0 194.2 jit_solution(10939244882465304126)
XLA Ops:
  0.0 2.4 %copy.26.w_ref = bf16[4096,64]{1,0:T(8,128)(2,1)} copy(bf16[4096,64]{0,1:T(8,128)(2,1)} %param.15) | data formatting | bytes 1048576 | tf_op args[5]
  2.4 115.3 %shard_map.100 = bf16[768,128]{1,0:T(8,128)(2,1)} custom-call(bf16[48,4096]{1,0:T(8,128)(2,1)} %bitcast.24, bf16[48,4096]{1,0:T(8,128)(2,1)} %bitcast.25, bf16[48,4096]{1,0:T(8,128)(2,1)} %bitcast.26, bf16[4096,64]{1,0:T(8,128)(2,1)} %copy.26.w_ref), custom_call_target="tpu_custom_call" | custom-call | tf_op jit(solution)/shard_map/pallas_call | solution.py:210
  117.7 1.7 reshape.33
  119.5 11.7 %all-to-all-start = ((bf16[16,2,1536]{2,1,0:T(2,128)(2,1)}), bf16[16,2,1536]{2,1,0:T(2,128)(2,1)S(1)}, u32[]{:S(2)}, u32[]{:S(2)}) async-start(bf16[16,2,1536]{2,1,0:T(2,128)(2,1)} %reshape.33), calls=%async_computation | async-start | bytes 196608 | tf_op jit(solution)/shard_map/all_to_all | solution.py:240
  131.2 11.7 %all-to-all-done = bf16[16,2,1536]{2,1,0:T(2,128)(2,1)S(1)} async-done(((bf16[16,2,1536]{2,1,0:T(2,128)(2,1)}), bf16[16,2,1536]{2,1,0:T(2,128)(2,1)S(1)}, u32[]{:S(2)}, u32[]{:S(2)}) %all-to-all-start) | async-done | bytes 98336 | tf_op jit(solution)/shard_map/all_to_all | solution.py:240
  143.2 8.4 %collective-permute-start = (f32[48,64]{1,0:T(8,128)S(1)}, f32[48,64]{1,0:T(8,128)S(1)}, u32[]{:S(2)}, u32[]{:S(2)}) collective-permute-start(f32[48,64]{1,0:T(8,128)S(1)} %convert_reduce_fusion), channel_id=1, source_target_pairs={{0,1},{1,0},{2,3},{3,2},{4,5},{5,4},{6,7},{7,6},{8,9},{9,8},{10,11... | collective-permute-start | bytes 36872 | tf_op jit(solution)/shard_map/ppermute | solution.py:245
  151.6 0.6 copy-done.3
  152.3 0.6 copy-done.4
  153.2 0.7 copy.27
  153.9 0.5 broadcast.6
  154.4 8.8 %reduce = bf16[1536,2]{1,0:T(8,128)(2,1)S(1)} reduce(bf16[1536,1,2]{2,1,0:T(2,128)(2,1)S(1)} %bitcast.18, bf16[]{:T(256)} %broadcast.6), dimensions={1}, to_apply=%bitcast.12.reduce_sub_computation | reduce | bytes 12290
  163.2 1.1 reshape.35
  164.3 4.7 %all-to-all-start.1 = ((bf16[8,2,192]{2,1,0:T(2,128)(2,1)}), bf16[8,2,192]{2,1,0:T(2,128)(2,1)S(1)}, u32[]{:S(2)}, u32[]{:S(2)}) async-start(bf16[8,2,192]{2,1,0:T(2,128)(2,1)} %reshape.35), calls=%async_computation.1 | async-start | bytes 16384 | tf_op jit(solution)/shard_map/all_to_all | solution.py:299
  169.0 6.6 %all-to-all-done.1 = bf16[8,2,192]{2,1,0:T(2,128)(2,1)S(1)} async-done(((bf16[8,2,192]{2,1,0:T(2,128)(2,1)}), bf16[8,2,192]{2,1,0:T(2,128)(2,1)S(1)}, u32[]{:S(2)}, u32[]{:S(2)}) %all-to-all-start.1) | async-done | bytes 6176 | tf_op jit(solution)/shard_map/all_to_all | solution.py:299
  175.6 0.9 reshape.36
  177.2 2.8 %collective-permute-start.1 = (bf16[6,1,6,16]{3,0,2,1:T(8,128)(2,1)S(1)}, bf16[6,1,6,16]{3,0,2,1:T(8,128)(2,1)S(1)}, u32[]{:S(2)}, u32[]{:S(2)}) collective-permute-start(bf16[6,1,6,16]{3,0,2,1:T(8,128)(2,1)S(1)} %get-tuple-element.39), channel_id=1, source_target_pairs={{0,16},{16,32},{32,48},{48,64},{64,80},{80,96},{96,112},{112,128},... | collective-permute-start | bytes 3464 | tf_op jit(solution)/shard_map/ppermute | solution.py:255
  180.1 1.3 collective-permute-start.2
  181.6 3.0 %collective-permute-done.2 = bf16[6,1,6,16]{3,0,2,1:T(8,128)(2,1)S(1)} collective-permute-done((bf16[6,1,6,16]{3,0,2,1:T(8,128)(2,1)S(1)}, bf16[6,1,6,16]{3,0,2,1:T(8,128)(2,1)S(1)}, u32[]{:S(2)}, u32[]{:S(2)}) %collective-permute-start.2) | collective-permute-done | bytes 1184 | tf_op jit(solution)/shard_map/ppermute | solution.py:256
  184.6 2.3 %collective-permute-start.3 = (bf16[6,6,1,16]{3,0,2,1:T(8,128)(2,1)S(1)}, bf16[6,6,1,16]{3,0,2,1:T(8,128)(2,1)S(1)}, u32[]{:S(2)}, u32[]{:S(2)}) collective-permute-start(bf16[6,6,1,16]{3,0,2,1:T(8,128)(2,1)S(1)} %get-tuple-element.26), channel_id=1, source_target_pairs={{0,2},{2,4},{4,6},{6,8},{8,10},{10,12},{12,14},{1,3},{3,5},{5,7},{... | collective-permute-start | bytes 3464 | tf_op jit(solution)/shard_map/ppermute | solution.py:255
  186.9 1.3 collective-permute-start.4
  188.3 3.1 %collective-permute-done.4 = bf16[6,6,1,16]{3,0,2,1:T(8,128)(2,1)S(1)} collective-permute-done((bf16[6,6,1,16]{3,0,2,1:T(8,128)(2,1)S(1)}, bf16[6,6,1,16]{3,0,2,1:T(8,128)(2,1)S(1)}, u32[]{:S(2)}, u32[]{:S(2)}) %collective-permute-start.4) | collective-permute-done | bytes 1184 | tf_op jit(solution)/shard_map/ppermute | solution.py:256
  191.5 1.0 concatenate.48
  192.6 0.6 copy-done.2
  193.5 0.7 copy.31
  (36 shorter events, 2.1 us)
Async XLA Ops:
  0.0 192.6 %copy-start = (bf16[3,3,3,16,384]{4,3,2,1,0:T(8,128)(2,1)S(1)}, bf16[3,3,3,16,384]{4,3,2,1,0:T(8,128)(2,1)}, u32[]{:S(2)}) copy-start(bf16[3,3,3,16,384]{4,3,2,1,0:T(8,128)(2,1)} %param.18) | copy-start | bytes 995332
  119.5 23.4 %all-to-all-start = ((bf16[16,2,1536]{2,1,0:T(2,128)(2,1)}), bf16[16,2,1536]{2,1,0:T(2,128)(2,1)S(1)}, u32[]{:S(2)}, u32[]{:S(2)}) async-start(bf16[16,2,1536]{2,1,0:T(2,128)(2,1)} %reshape.33), calls=%async_computation | async-start | bytes 196608 | tf_op jit(solution)/shard_map/all_to_all | solution.py:240
  143.1 8.5 %copy-start.5 = (s32[48]{0:T(128)S(1)}, s32[48]{0:T(128)}, u32[]{:S(2)}) copy-start(s32[48]{0:T(128)} %param.14) | copy-start | bytes 580
  143.1 9.9 %copy-start.1 = (f32[48,64]{1,0:T(8,128)S(1)}, f32[48,64]{1,0:T(8,128)}, u32[]{:S(2)}) copy-start(f32[48,64]{1,0:T(8,128)} %param.13) | copy-start | bytes 36868
  143.2 9.8 %collective-permute-start = (f32[48,64]{1,0:T(8,128)S(1)}, f32[48,64]{1,0:T(8,128)S(1)}, u32[]{:S(2)}, u32[]{:S(2)}) collective-permute-start(f32[48,64]{1,0:T(8,128)S(1)} %convert_reduce_fusion), channel_id=1, source_target_pairs={{0,1},{1,0},{2,3},{3,2},{4,5},{5,4},{6,7},{7,6},{8,9},{9,8},{10,11... | collective-permute-start | bytes 36872 | tf_op jit(solution)/shard_map/ppermute | solution.py:245
  151.6 0.7 copy-start.3
  152.2 0.7 copy-start.4
  164.3 11.3 %all-to-all-start.1 = ((bf16[8,2,192]{2,1,0:T(2,128)(2,1)}), bf16[8,2,192]{2,1,0:T(2,128)(2,1)S(1)}, u32[]{:S(2)}, u32[]{:S(2)}) async-start(bf16[8,2,192]{2,1,0:T(2,128)(2,1)} %reshape.35), calls=%async_computation.1 | async-start | bytes 16384 | tf_op jit(solution)/shard_map/all_to_all | solution.py:299
  177.2 4.3 %collective-permute-start.1 = (bf16[6,1,6,16]{3,0,2,1:T(8,128)(2,1)S(1)}, bf16[6,1,6,16]{3,0,2,1:T(8,128)(2,1)S(1)}, u32[]{:S(2)}, u32[]{:S(2)}) collective-permute-start(bf16[6,1,6,16]{3,0,2,1:T(8,128)(2,1)S(1)} %get-tuple-element.39), channel_id=1, source_target_pairs={{0,16},{16,32},{32,48},{48,64},{64,80},{80,96},{96,112},{112,128},... | collective-permute-start | bytes 3464 | tf_op jit(solution)/shard_map/ppermute | solution.py:255
  180.1 4.5 %collective-permute-start.2 = (bf16[6,1,6,16]{3,0,2,1:T(8,128)(2,1)S(1)}, bf16[6,1,6,16]{3,0,2,1:T(8,128)(2,1)S(1)}, u32[]{:S(2)}, u32[]{:S(2)}) collective-permute-start(bf16[6,1,6,16]{3,0,2,1:T(8,128)(2,1)S(1)} %get-tuple-element.40), channel_id=1, source_target_pairs={{16,0},{32,16},{48,32},{64,48},{80,64},{96,80},{112,96},{128,112},... | collective-permute-start | bytes 3464 | tf_op jit(solution)/shard_map/ppermute | solution.py:256
  184.6 3.7 %collective-permute-start.3 = (bf16[6,6,1,16]{3,0,2,1:T(8,128)(2,1)S(1)}, bf16[6,6,1,16]{3,0,2,1:T(8,128)(2,1)S(1)}, u32[]{:S(2)}, u32[]{:S(2)}) collective-permute-start(bf16[6,6,1,16]{3,0,2,1:T(8,128)(2,1)S(1)} %get-tuple-element.26), channel_id=1, source_target_pairs={{0,2},{2,4},{4,6},{6,8},{8,10},{10,12},{12,14},{1,3},{3,5},{5,7},{... | collective-permute-start | bytes 3464 | tf_op jit(solution)/shard_map/ppermute | solution.py:255
  186.9 4.5 %collective-permute-start.4 = (bf16[6,6,1,16]{3,0,2,1:T(8,128)(2,1)S(1)}, bf16[6,6,1,16]{3,0,2,1:T(8,128)(2,1)S(1)}, u32[]{:S(2)}, u32[]{:S(2)}) collective-permute-start(bf16[6,6,1,16]{3,0,2,1:T(8,128)(2,1)S(1)} %get-tuple-element.25), channel_id=1, source_target_pairs={{2,0},{4,2},{6,4},{8,6},{10,8},{12,10},{14,12},{3,1},{5,3},{7,5},{... | collective-permute-start | bytes 3464 | tf_op jit(solution)/shard_map/ppermute | solution.py:256
  192.6 0.7 copy-start.2

commit v2 on v1

v2 whole, which is shorter than its diff:
```python
import functools
import math

import jax
import jax.numpy as jnp
from jax import lax
from jax.experimental import pallas as pl
from jax.experimental.pallas import tpu as pltpu
from jax.sharding import PartitionSpec as P

HDIM = 128
ZCH = 16
COLS_DEV = 3
ROW_PAD = 8
TAP_LANES = 256
GUIDE = 5.0
NOISE_LEVEL = 0.5
MESH = pl.DeviceIdType.MESH
EXP_SCALE = math.log2(math.e) / math.sqrt(HDIM)


def exchange_kernel(
    nz, nx, q_ref, k_ref, v_ref, w_ref, noisy_ref, order_ref, std_ref, mean_ref, taps_ref, bias_ref, out_ref,
    vsend, gx, qx, vt, top, total, acc, wide, vout, vin, psend, tile, halo, grid, xcol, wexp, final,
    zsend, zrecv, xsend, xrecv, vsent, vrecv, psent, precv,
):
    seq = lax.axis_index("seq")
    blk = lax.axis_index("blk")
    cfg = lax.axis_index("cfg")
    tok = q_ref.shape[0]
    rows = gx.shape[2]
    part = rows // 2
    patch = w_ref.shape[0]
    frames = nx // 2
    few = tok // 2
    hops = nx // 2
    right = lax.rem(blk + 1, nx)
    left = lax.rem(blk + nx - 1, nx)

    barrier = pltpu.get_barrier_semaphore()

    def greet(s, b):
        for c in range(2):
            pl.semaphore_signal(
                barrier, inc=1, device_id={"seq": s, "blk": b, "cfg": c}, device_id_type=MESH
            )

    def greet_seq(d, _):
        greet(lax.rem(seq + d, nz), blk)
        return 0

    def greet_blk(d, _):
        b = lax.rem(blk + d, nx)
        for near in (0, 1, nz - 1):
            greet(lax.rem(seq + near, nz), b)
        return 0

    xcol[...] = jnp.zeros(xcol.shape, jnp.float32)
    lax.fori_loop(1, nz, greet_seq, 0)
    lax.fori_loop(1, nx, greet_blk, 0)
    pl.semaphore_signal(barrier, inc=1, device_id={"cfg": 1 - cfg}, device_id_type=MESH)

    def project(s, _):
        both = []
        for h in range(2):
            at = pl.ds(pl.multiple_of((2 * s + h) * HDIM, HDIM), HDIM)
            both.append(
                lax.dot_general(
                    v_ref[:, at], w_ref[:, at], (((1,), (1,)), ((), ())),
                    preferred_element_type=jnp.float32,
                )
            )
        vsend[s] = jnp.concatenate(both, axis=1).astype(jnp.bfloat16)
        return 0

    lax.fori_loop(0, nz, project, 0)
    wexp[...] = jnp.zeros(wexp.shape, jnp.bfloat16)
    for step_t in range(3):
        for step_y in range(3):
            taps = taps_ref[pl.ds((3 * step_t + step_y) * 3 * ZCH, 3 * ZCH), :]
            at = step_t * TAP_LANES + step_y * 4 * ZCH
            wexp[0, pl.ds(at + ZCH, 3 * ZCH), :] = taps
            wexp[1, pl.ds(at, 3 * ZCH), :] = taps
    pl.semaphore_wait(barrier, 2 * (nz - 1) + 6 * (nx - 1) + 1)

    own_rows = pl.ds(pl.multiple_of(seq * tok, tok), tok)

    def columns(ref, s, h):
        return ref.at[:, pl.ds(pl.multiple_of((2 * s + h) * HDIM, HDIM), HDIM)]

    sources = (
        lambda s: columns(k_ref, s, 0),
        lambda s: vsend.at[s],
        lambda s: columns(q_ref, s, 0),
        lambda s: columns(k_ref, s, 1),
        lambda s: columns(q_ref, s, 1),
    )
    whole = (gx.at[0, blk], gx.at[1, blk], qx.at[0], gx.at[2, blk], qx.at[1])

    def spread(i):
        pltpu.make_async_copy(
            sources[i](seq), whole[i].at[own_rows, :], zrecv.at[i]
        ).start()

        def send(d, _):
            far = (d + 1) // 2
            peer = lax.rem(seq + jnp.where(lax.rem(d, 2) == 1, far, nz - far), nz)
            pltpu.make_async_remote_copy(
                src_ref=sources[i](peer),
                dst_ref=whole[i].at[own_rows, :],
                send_sem=zsend.at[i],
                recv_sem=zrecv.at[i],
                device_id={"seq": peer},
                device_id_type=MESH,
            ).start()
            return 0

        lax.fori_loop(1, nz, send, 0)

    def spread_done(i):
        pltpu.make_async_copy(whole[i], whole[i], zrecv.at[i]).wait()

    def ring(c, way, step, half):
        block = lax.rem(blk + (nx - step + 1 if way == 0 else step - 1), nx)
        piece = gx.at[c, block, pl.ds(half * part, part), :]
        return pltpu.make_async_remote_copy(
            src_ref=piece,
            dst_ref=piece,
            send_sem=xsend.at[c, way, step - 1, half],
            recv_sem=xrecv.at[c, way, step - 1, half],
            device_id={"blk": right if way == 0 else left},
            device_id_type=MESH,
        )

    def travels(way, step, half):
        return step < hops or (step == hops and way == half)

    def begin(c):
        for half in range(2):
            for way in range(2):
                if travels(way, 1, half):
                    ring(c, way, 1, half).start()

    def advance(c, step):
        for half in range(2):
            for way in range(2):
                if travels(way, step, half):
                    ring(c, way, step, half).wait_recv()
                    if travels(way, step + 1, half):
                        ring(c, way, step + 1, half).start()

    qtile = 256

    def attend(h, block):
        if h == 0:
            vt[block] = gx[1, block].T
        keys = gx[2 * h, block]
        values = vt[block, pl.ds(h * patch, patch), :]
        for t in range(rows // qtile):
            at = pl.ds(t * qtile, qtile)
            scores = lax.dot_general(
                keys, qx[h, at, :], (((1,), (1,)), ((), ())),
                preferred_element_type=jnp.float32,
            )
            old = top[h, :, at]
            new = jnp.maximum(old, jnp.max(scores, axis=0, keepdims=True))
            expo = jnp.exp2(scores * EXP_SCALE - new * EXP_SCALE)
            factor = jnp.exp2((old - new) * EXP_SCALE)
            top[h, :, at] = new
            total[h, :, at] = total[h, :, at] * factor + jnp.sum(expo, axis=0, keepdims=True)
            acc[h, :, at] = acc[h, :, at] * factor + jnp.dot(
                values, expo.astype(jnp.bfloat16), preferred_element_type=jnp.float32
            )

    def near(h, step):
        def one(way, _):
            block = lax.rem(blk + jnp.where(way == 0, nx - step, step), nx)
            attend(h, block)
            return 0

        lax.fori_loop(0, 2, one, 0)

    for i in range(5):
        spread(i)
    top[...] = jnp.full(top.shape, -1e30, jnp.float32)
    total[...] = jnp.zeros(total.shape, jnp.float32)
    acc[...] = jnp.zeros(acc.shape, jnp.float32)

    spread_done(0)
    begin(0)
    for step in range(1, hops - 1):
        advance(0, step)
    spread_done(1)
    begin(1)
    for step in range(hops - 1, hops + 1):
        advance(0, step)
    spread_done(2)
    attend(0, blk)
    for step in range(1, hops):
        advance(1, step)
        if step == hops - 1:
            spread_done(3)
            begin(2)
        near(0, step)
    advance(1, hops)
    attend(0, lax.rem(blk + hops, nx))
    spread_done(4)
    attend(1, blk)
    for step in range(1, hops):
        advance(2, step)
        near(1, step)
    advance(2, hops)
    attend(1, lax.rem(blk + hops, nx))

    velocity = acc[0] / total[0] + acc[1] / total[1]
    velocity = velocity * jnp.where(cfg == 0, GUIDE, 1.0 - GUIDE)
    later = pltpu.roll(velocity, rows - few, 1)
    wide[...] = jnp.concatenate([velocity, later], axis=0).T

    def pack(s, _):
        vout[s] = wide[pl.ds(pl.multiple_of(s * tok, 16), few), :].astype(jnp.bfloat16)
        return 0

    lax.fori_loop(0, nz, pack, 0)
    slot = cfg * nz + seq

    def share(peer):
        return pltpu.make_async_remote_copy(
            src_ref=vout.at[peer],
            dst_ref=vin.at[slot],
            send_sem=vsent,
            recv_sem=vrecv,
            device_id={"seq": peer, "cfg": 1},
            device_id_type=MESH,
        )

    def send_share(d, _):
        far = nz // 2 - d // 2
        share(lax.rem(seq + jnp.where(lax.rem(d, 2) == 1, far, nz - far), nz)).start()
        return 0

    lax.fori_loop(1, nz, send_share, 0)

    @pl.when(cfg == 0)
    def _():
        share(seq).start()
        pltpu.make_async_copy(vout, vout, vsent).wait()

    def greater(target_cfg):
        return blk < frames if target_cfg == 0 else blk >= frames - 2

    @pl.when(cfg == 1)
    def _():
        pltpu.make_async_copy(vout.at[seq], vin.at[slot], vrecv).start()
        pltpu.make_async_copy(vin, vin, vrecv).wait()
        guided = jnp.sum(vin[...].astype(jnp.float32), axis=0)
        noisy = jnp.concatenate([noisy_ref[0:few, :], noisy_ref[few:tok, :]], axis=1)
        scale = jnp.concatenate([std_ref[...]] * (2 * patch // ZCH), axis=1)
        shift = jnp.concatenate([mean_ref[...]] * (2 * patch // ZCH), axis=1)
        pixels = (noisy - NOISE_LEVEL * guided) * scale + shift
        pixels = jnp.concatenate([pixels[:, :patch], pixels[:, patch:]], axis=0).astype(jnp.bfloat16)

        entry = lax.broadcasted_iota(jnp.int32, (patch, 2 * patch), 0)
        lane = lax.broadcasted_iota(jnp.int32, (patch, 2 * patch), 1)
        half = patch // 2
        spread_pixels = []
        for p in range(2):
            place = (
                (entry // half == lane // patch)
                & (entry % half == lane % half)
                & ((lane // half) % 2 == p)
            ).astype(jnp.bfloat16)
            spread_pixels.append(jnp.dot(pixels, place, preferred_element_type=jnp.float32))
        spread_pixels = jnp.concatenate(spread_pixels, axis=0).astype(jnp.bfloat16)
        slots = order_ref[...] - (blk * nz + seq) * tok
        slots = jnp.concatenate([slots, slots], axis=1)
        row = lax.broadcasted_iota(jnp.int32, (ROW_PAD * nx, 2 * tok), 0)
        token = lax.broadcasted_iota(jnp.int32, (ROW_PAD * nx, 2 * tok), 1)
        x = row % ROW_PAD
        column = COLS_DEV * (row // ROW_PAD) - 1 + (x + 1) // 2 + token // tok
        inside = (x < 2 * COLS_DEV) & (column >= 0) & (column < COLS_DEV * nx)
        for i in range(2):
            select = (inside & (slots == column + i * COLS_DEV * nx)).astype(jnp.bfloat16)
            picked = jnp.dot(select, spread_pixels, preferred_element_type=jnp.float32)
            psend[:, :, i * 2 * patch : (i + 1) * 2 * patch] = picked.reshape(
                nx, ROW_PAD, 2 * patch
            ).astype(jnp.bfloat16)

        above = lax.rem(seq + nz - 1, nz)
        below = lax.rem(seq + 1, nz)
        pieces = (
            (0, pl.ds(0, 4 * patch), tile.at[blk], seq),
            (1, pl.ds(2 * patch, 2 * patch), halo.at[blk, 0], below),
            (1, pl.ds(0, 2 * patch), halo.at[blk, 1], above),
        )
        for c in range(2):

            @pl.when(greater(c))
            def _():
                def send_pieces(d, _):
                    b = lax.rem(blk + d, nx)
                    for kind, at, there, s in pieces:
                        pltpu.make_async_remote_copy(
                            src_ref=psend.at[b, :, at],
                            dst_ref=there,
                            send_sem=psent.at[c, kind],
                            recv_sem=precv.at[kind],
                            device_id={"seq": s, "blk": b, "cfg": c},
                            device_id_type=MESH,
                        ).start()
                    return 0

                lax.fori_loop(1, nx, send_pieces, 0)
                for kind, at, there, s in pieces:
                    if c == 1 and kind == 0:
                        pltpu.make_async_copy(psend.at[blk, :, at], there, precv.at[0]).start()
                    else:
                        pltpu.make_async_remote_copy(
                            src_ref=psend.at[blk, :, at],
                            dst_ref=there,
                            send_sem=psent.at[c, kind],
                            recv_sem=precv.at[kind],
                            device_id={"seq": s, "cfg": c},
                            device_id_type=MESH,
                        ).start()

    for c in range(2):

        @pl.when(cfg == c)
        def _():
            arrived = pl.ds(0, frames) if c == 0 else pl.ds(frames - 2, frames + 2)
            pltpu.make_async_copy(tile.at[arrived], tile.at[arrived], precv.at[0]).wait()
            pltpu.make_async_copy(halo.at[arrived], halo.at[arrived], precv.at[1]).wait()

    def line(g, _):
        frame = cfg * frames - 2 + g
        known = frame >= 0
        frame = jnp.maximum(frame, 0)
        upper = halo[frame, 0].astype(jnp.float32)[:, patch:]
        lower = halo[frame, 1].astype(jnp.float32)[:, :patch]
        upper = jnp.where(known & (seq > 0), upper, 0.0)
        lower = jnp.where(known & (seq < nz - 1), lower, 0.0)
        middle = jnp.where(known, tile[frame].astype(jnp.float32), 0.0)
        grid[g] = jnp.concatenate([upper, middle, lower], axis=1)
        return 0

    lax.fori_loop(0, frames + 2, line, 0)
    for f in range(frames):
        for y in range(4):
            for step_t in range(3):
                xcol[pl.ds((4 * f + y) * ROW_PAD, ROW_PAD), pl.ds(step_t * TAP_LANES, 3 * patch)] = grid[
                    f + step_t, :, pl.ds(y * patch, 3 * patch)
                ]
    odd = lax.broadcasted_iota(jnp.int32, xcol.shape, 0) % 2 == 1
    features = bias_ref[...]
    for parity in range(2):
        kept = jnp.where(odd if parity else ~odd, xcol[...], 0.0).astype(jnp.bfloat16)
        features = features + jnp.dot(kept, wexp[parity], preferred_element_type=jnp.float32)
    wide_x = 2 * COLS_DEV
    to = lax.broadcasted_iota(jnp.int32, (frames * wide_x * 4, xcol.shape[0]), 0)
    at = lax.broadcasted_iota(jnp.int32, (frames * wide_x * 4, xcol.shape[0]), 1)
    source = ((to // (4 * wide_x)) * 4 + to % 4) * ROW_PAD + (to // 4) % wide_x
    order = (source == at).astype(jnp.bfloat16)
    final[...] = jnp.dot(order, features.astype(jnp.bfloat16), preferred_element_type=jnp.float32)
    for f in range(frames):
        for x in range(wide_x):
            out_ref[f, x] = final[pl.ds((f * wide_x + x) * 4, 4), :].astype(jnp.bfloat16)

    @pl.when(cfg == 1)
    def _():
        sent = vout.at[pl.ds(0, nz - 1)]
        pltpu.make_async_copy(sent, sent, vsent).wait()
        for c in range(2):

            @pl.when(greater(c))
            def _():
                tiles = psend.at[pl.ds(0, nx - c)]
                pltpu.make_async_copy(tiles, tiles, psent.at[c, 0]).wait()
                pltpu.make_async_copy(psend, psend, psent.at[c, 1]).wait()

    for i in range(5):
        sent = whole[i].at[pl.ds(0, rows - tok), :]
        pltpu.make_async_copy(sent, sent, zsend.at[i]).wait()
    for c in range(3):
        for step in range(1, hops + 1):
            for half in range(2):
                for way in range(2):
                    if travels(way, step, half):
                        ring(c, way, step, half).wait_send()


def local(
    queries,
    key_states,
    value_states,
    noisy_latents,
    patch_order,
    head_weight,
    latent_std,
    latent_mean,
    conv_weight,
    conv_bias,
):
    nz = lax.axis_size("seq")
    nx = lax.axis_size("blk")
    tok = queries.shape[1]
    rows = nz * tok
    patch = head_weight.shape[1]
    wide = conv_weight.shape[4]
    frames = nx // 2
    pixels = 4 * frames * ROW_PAD
    vmem = pl.BlockSpec(memory_space=pltpu.VMEM)
    features = pl.pallas_call(
        functools.partial(exchange_kernel, nz, nx),
        out_shape=jax.ShapeDtypeStruct((frames, 2 * COLS_DEV, 4, wide), jnp.bfloat16),
        in_specs=[vmem] * 10,
        out_specs=vmem,
        scratch_shapes=[
            pltpu.VMEM((nz, tok, 2 * patch), jnp.bfloat16),
            pltpu.VMEM((3, nx, rows, HDIM), jnp.bfloat16),
            pltpu.VMEM((2, rows, HDIM), jnp.bfloat16),
            pltpu.VMEM((nx, 2 * patch, rows), jnp.bfloat16),
            pltpu.VMEM((2, 1, rows), jnp.float32),
            pltpu.VMEM((2, 1, rows), jnp.float32),
            pltpu.VMEM((2, patch, rows), jnp.float32),
            pltpu.VMEM((rows, 2 * patch), jnp.float32),
            pltpu.VMEM((nz, tok // 2, 2 * patch), jnp.bfloat16),
            pltpu.VMEM((2 * nz, tok // 2, 2 * patch), jnp.bfloat16),
            pltpu.VMEM((nx, ROW_PAD, 4 * patch), jnp.bfloat16),
            pltpu.VMEM((nx, ROW_PAD, 4 * patch), jnp.bfloat16),
            pltpu.VMEM((nx, 2, ROW_PAD, 2 * patch), jnp.bfloat16),
            pltpu.VMEM((frames + 2, ROW_PAD, 6 * patch), jnp.float32),
            pltpu.VMEM((pixels, 3 * TAP_LANES), jnp.float32),
            pltpu.VMEM((2, 3 * TAP_LANES, wide), jnp.bfloat16),
            pltpu.VMEM((8 * frames * COLS_DEV, wide), jnp.float32),
            pltpu.SemaphoreType.DMA((5,)),
            pltpu.SemaphoreType.DMA((5,)),
            pltpu.SemaphoreType.DMA((3, 2, nx // 2, 2)),
            pltpu.SemaphoreType.DMA((3, 2, nx // 2, 2)),
            pltpu.SemaphoreType.DMA,
            pltpu.SemaphoreType.DMA,
            pltpu.SemaphoreType.DMA((2, 2)),
            pltpu.SemaphoreType.DMA((2,)),
        ],
        compiler_params=pltpu.CompilerParams(collective_id=0, has_side_effects=True),
    )(
        queries[0],
        key_states[0],
        value_states[0],
        head_weight.T,
        noisy_latents,
        patch_order.reshape(1, tok),
        latent_std.reshape(1, ZCH),
        latent_mean.reshape(1, ZCH),
        conv_weight.reshape(27 * ZCH, wide),
        conv_bias.reshape(1, wide),
    )
    return features.transpose(0, 2, 1, 3)


def solution(mesh):
    in_specs = (
        P("cfg", ("prompt", "blk", "seq"), None),
        P("cfg", ("prompt", "blk", "seq"), None),
        P("cfg", ("prompt", "blk", "seq"), None),
        P(("prompt", "blk", "seq"), None),
        P(("prompt", "blk", "seq")),
        P(),
        P(),
        P(),
        P(),
        P(),
    )
    out_specs = P(("prompt", "cfg"), "seq", "blk", None)
    return jax.shard_map(local, mesh=mesh, in_specs=in_specs, out_specs=out_specs, check_vma=False)
```

time: 197 us -> 144 us (0.73); the launches traced: 194 us -> 144 us
  starting transfers between devices: 32.5 us -> 0 us
  Pallas kernels: 115 us -> 141 us
  waiting for transfers between devices: 24.4 us -> 0 us
  local copies, waits for them, and re-layouts: 12.3 us -> 2.79 us
  other arithmetic: 8.99 us -> 0 us
    pallas_call x1, Pallas kernels: 115 us -> 141 us  [local(): pl.pallas_call(functools.partial(exchange_kernel, nz, nx), out_shape=jax....]
    all_to_all x2 -> x0, waiting for transfers between devices: 18.3 us -> none  [the longest x1 11.7 us: sum_at_owner(): lax.all_to_all(split_up(array, dim, devices), axis, 0, 0, tiled=True)]
    all_to_all x2 -> x0, starting transfers between devices: 16.4 us -> none  [the longest x1 11.7 us: sum_at_owner(): lax.all_to_all(split_up(array, dim, devices), axis, 0, 0, tiled=True)]
    ppermute x5 -> x0, starting transfers between devices: 16.2 us -> none  [the longest x1 8.39 us: partner(): lax.ppermute(array, axis, [(i, i ^ 1 << apart) for i in range(lax.axis_si...]
    unnamed x1 -> x0, other arithmetic: 8.81 us -> none
    unnamed x18 -> x3, local copies, waits for them, and re-layouts: 8.7 us -> 2.22 us
    ppermute x5 -> x0, waiting for transfers between devices: 6.06 us -> none  [the longest x2 6.05 us: padded(): after = lax.ppermute(first, axis, down)]
  transfers between devices with their start and end apart: 7 -> 0, of which waited for: 4 -> 0; matrix products, arithmetic and copies ran while one was open for 0% -> 0% of each run, Pallas kernels for 0% -> 0%
where the time goes in v2:
time: 144 us
  Pallas kernels  141 us (98%)
  local copies, waits for them, and re-layouts  2.79 us (2%)
    pallas_call x1, Pallas kernels, local(): pl.pallas_call(functools.partial(exchange_kernel, nz, nx), out_shape=jax....  141 us

profile of v2, /device:TPU:65, one launch (start us, length us, event | category | flops | bytes accessed | tf_op | source)
XLA Modules:
  0.0 143.8 jit_solution(2171409899200974798)
XLA Ops:
  0.0 0.0 copy-start
  0.0 0.7 copy-done
  0.7 0.6 reshape.19.bias_ref
  1.2 141.0 %shard_map.100 = bf16[4,6,4,384]{3,2,1,0:T(4,128)(2,1)} custom-call(bf16[48,4096]{1,0:T(8,128)(2,1)} %bitcast.10, bf16[48,4096]{1,0:T(8,128)(2,1)} %bitcast.11, bf16[48,4096]{1,0:T(8,128)(2,1)} %bitcast.12, bf16[64,4096]{1,0:T(8,128)(2,1)} %bitcast.9, f32[48,64]{1,0:T(8,128)} %noisy_ref.1, s32[1,48]{1,0:T(1,128)} %bitcast.15, f32[1,16]{1,0:T(1,128)} %bitcast.16, ...), custom_call_target="tpu_custom_call" | custom-call | tf_op jit(solution)/shard_map/pallas_call | solution.py:413
  142.2 1.5 %copy.12 = bf16[4,4,6,384]{3,1,2,0:T(4,128)(2,1)} copy(bf16[4,4,6,384]{3,1,2,0:T(4,128)(2,1)} %bitcast.14) | data formatting | bytes 147456
Async XLA Ops:
  0.0 0.7 copy-start

commit v3 on v2

--- a/solution.py
+++ b/solution.py
@@ -13,6 +13,7 @@
 COLS_DEV = 3
 ROW_PAD = 8
 TAP_LANES = 256
+ONES = 16
 GUIDE = 5.0
 NOISE_LEVEL = 0.5
 MESH = pl.DeviceIdType.MESH
@@ -21,7 +22,7 @@
 
 def exchange_kernel(
     nz, nx, q_ref, k_ref, v_ref, w_ref, noisy_ref, order_ref, std_ref, mean_ref, taps_ref, bias_ref, out_ref,
-    vsend, gx, qx, vt, top, total, acc, wide, vout, vin, psend, tile, halo, grid, xcol, wexp, final,
+    vsend, gx, qx, vt, top, acc, wide, vout, vin, psend, tile, halo, grid, xcol, wexp, final,
     zsend, zrecv, xsend, xrecv, vsent, vrecv, psent, precv,
 ):
     seq = lax.axis_index("seq")
@@ -55,10 +56,11 @@
             greet(lax.rem(seq + near, nz), b)
         return 0
 
-    xcol[...] = jnp.zeros(xcol.shape, jnp.float32)
     lax.fori_loop(1, nz, greet_seq, 0)
     lax.fori_loop(1, nx, greet_blk, 0)
     pl.semaphore_signal(barrier, inc=1, device_id={"cfg": 1 - cfg}, device_id_type=MESH)
+
+    pl.semaphore_wait(barrier, 2 * (nz - 1) + 6 * (nx - 1) + 1)
 
     def project(s, _):
         both = []
@@ -73,41 +75,34 @@
         vsend[s] = jnp.concatenate(both, axis=1).astype(jnp.bfloat16)
         return 0
 
-    lax.fori_loop(0, nz, project, 0)
-    wexp[...] = jnp.zeros(wexp.shape, jnp.bfloat16)
-    for step_t in range(3):
-        for step_y in range(3):
-            taps = taps_ref[pl.ds((3 * step_t + step_y) * 3 * ZCH, 3 * ZCH), :]
-            at = step_t * TAP_LANES + step_y * 4 * ZCH
-            wexp[0, pl.ds(at + ZCH, 3 * ZCH), :] = taps
-            wexp[1, pl.ds(at, 3 * ZCH), :] = taps
-    pl.semaphore_wait(barrier, 2 * (nz - 1) + 6 * (nx - 1) + 1)
-
-    own_rows = pl.ds(pl.multiple_of(seq * tok, tok), tok)
-
-    def columns(ref, s, h):
-        return ref.at[:, pl.ds(pl.multiple_of((2 * s + h) * HDIM, HDIM), HDIM)]
-
-    sources = (
-        lambda s: columns(k_ref, s, 0),
-        lambda s: vsend.at[s],
-        lambda s: columns(q_ref, s, 0),
-        lambda s: columns(k_ref, s, 1),
-        lambda s: columns(q_ref, s, 1),
+    def columns(ref, first, count, s, h):
+        return ref.at[pl.ds(first, count), pl.ds(pl.multiple_of((2 * s + h) * HDIM, HDIM), HDIM)]
+
+    def half_of(c, half):
+        there = gx.at[c, blk, pl.ds(half * part, part), :]
+        if c == 1:
+            return lambda s: vsend.at[s, pl.ds(half * few, few), :], there, few
+        return lambda s: columns(k_ref, half * few, few, s, c // 2), there, few
+
+    def query_of(h):
+        return lambda s: columns(q_ref, 0, tok, s, h), qx.at[h], tok
+
+    parcels = (
+        half_of(0, 0), half_of(0, 1), half_of(1, 0), half_of(1, 1), query_of(0),
+        half_of(2, 0), half_of(2, 1), query_of(1),
     )
-    whole = (gx.at[0, blk], gx.at[1, blk], qx.at[0], gx.at[2, blk], qx.at[1])
 
     def spread(i):
-        pltpu.make_async_copy(
-            sources[i](seq), whole[i].at[own_rows, :], zrecv.at[i]
-        ).start()
+        source, whole, count = parcels[i]
+        there = whole.at[pl.ds(pl.multiple_of(seq * count, 8), count), :]
+        pltpu.make_async_copy(source(seq), there, zrecv.at[i]).start()
 
         def send(d, _):
-            far = (d + 1) // 2
+            far = nz // 2 - d // 2
             peer = lax.rem(seq + jnp.where(lax.rem(d, 2) == 1, far, nz - far), nz)
             pltpu.make_async_remote_copy(
-                src_ref=sources[i](peer),
-                dst_ref=whole[i].at[own_rows, :],
+                src_ref=source(peer),
+                dst_ref=there,
                 send_sem=zsend.at[i],
                 recv_sem=zrecv.at[i],
                 device_id={"seq": peer},
@@ -118,7 +113,8 @@
         lax.fori_loop(1, nz, send, 0)
 
     def spread_done(i):
-        pltpu.make_async_copy(whole[i], whole[i], zrecv.at[i]).wait()
+        whole = parcels[i][1]
+        pltpu.make_async_copy(whole, whole, zrecv.at[i]).wait()
 
     def ring(c, way, step, half):
         block = lax.rem(blk + (nx - step + 1 if way == 0 else step - 1), nx)
@@ -135,84 +131,120 @@
     def travels(way, step, half):
         return step < hops or (step == hops and way == half)
 
-    def begin(c):
+    def begin(c, half):
+        for way in range(2):
+            if travels(way, 1, half):
+                ring(c, way, 1, half).start()
+
+    def advance(c, step, half, way):
+        if travels(way, step, half):
+            ring(c, way, step, half).wait_recv()
+            if travels(way, step + 1, half):
+                ring(c, way, step + 1, half).start()
+
+    def advance_all(c, step):
         for half in range(2):
             for way in range(2):
-                if travels(way, 1, half):
-                    ring(c, way, 1, half).start()
-
-    def advance(c, step):
-        for half in range(2):
-            for way in range(2):
-                if travels(way, step, half):
-                    ring(c, way, step, half).wait_recv()
-                    if travels(way, step + 1, half):
-                        ring(c, way, step + 1, half).start()
-
-    qtile = 256
-
-    def attend(h, block):
+                advance(c, step, half, way)
+
+    qtile = rows // 2
+
+    def attend(h, blocks):
         if h == 0:
-            vt[block] = gx[1, block].T
-        keys = gx[2 * h, block]
-        values = vt[block, pl.ds(h * patch, patch), :]
-        for t in range(rows // qtile):
-            at = pl.ds(t * qtile, qtile)
-            scores = lax.dot_general(
-                keys, qx[h, at, :], (((1,), (1,)), ((), ())),
+            for block in blocks:
+                turned = gx[1, block].T
+                for g in range(2):
+                    vt[block, g, pl.ds(0, patch), :] = turned[g * patch : (g + 1) * patch, :]
+        items = [(block, t) for block in blocks for t in range(rows // qtile)]
+
+        def scores_of(block, t):
+            return lax.dot_general(
+                gx[2 * h, block], qx[h, pl.ds(t * qtile, qtile), :], (((1,), (1,)), ((), ())),
                 preferred_element_type=jnp.float32,
             )
+
+        ahead = len(blocks)
+        ready = [scores_of(*item) for item in items[:ahead]]
+        for n, (block, t) in enumerate(items):
+            if n + ahead < len(items):
+                ready.append(scores_of(*items[n + ahead]))
+            scores = ready.pop(0)
+            at = pl.ds(t * qtile, qtile)
             old = top[h, :, at]
             new = jnp.maximum(old, jnp.max(scores, axis=0, keepdims=True))
-            expo = jnp.exp2(scores * EXP_SCALE - new * EXP_SCALE)
+            expo = jnp.exp2(scores * EXP_SCALE - new * EXP_SCALE).astype(jnp.bfloat16)
             factor = jnp.exp2((old - new) * EXP_SCALE)
             top[h, :, at] = new
-            total[h, :, at] = total[h, :, at] * factor + jnp.sum(expo, axis=0, keepdims=True)
             acc[h, :, at] = acc[h, :, at] * factor + jnp.dot(
-                values, expo.astype(jnp.bfloat16), preferred_element_type=jnp.float32
+                vt[block, h], expo, preferred_element_type=jnp.float32
             )
 
-    def near(h, step):
-        def one(way, _):
-            block = lax.rem(blk + jnp.where(way == 0, nx - step, step), nx)
-            attend(h, block)
-            return 0
-
-        lax.fori_loop(0, 2, one, 0)
-
-    for i in range(5):
+    def behind(step):
+        return lax.rem(blk + nx - step, nx)
+
+    def beyond(step):
+        return lax.rem(blk + step, nx)
+
+    spread(0)
+    spread(1)
+    lax.fori_loop(0, nz, project, 0)
+    for i in range(2, len(parcels)):
         spread(i)
     top[...] = jnp.full(top.shape, -1e30, jnp.float32)
-    total[...] = jnp.zeros(total.shape, jnp.float32)
     acc[...] = jnp.zeros(acc.shape, jnp.float32)
+    vt[:, :, pl.ds(patch, vt.shape[2] - patch), :] = jnp.ones(
+        (nx, 2, vt.shape[2] - patch, rows), jnp.bfloat16
+    )
+    xcol[...] = jnp.zeros(xcol.shape, jnp.float32)
+    wexp[...] = jnp.zeros(wexp.shape, jnp.bfloat16)
+    for step_t in range(3):
+        for step_y in range(3):
+            taps = taps_ref[pl.ds((3 * step_t + step_y) * 3 * ZCH, 3 * ZCH), :]
+            at = step_t * TAP_LANES + step_y * 4 * ZCH
+            wexp[0, pl.ds(at + ZCH, 3 * ZCH), :] = taps
+            wexp[1, pl.ds(at, 3 * ZCH), :] = taps
 
     spread_done(0)
-    begin(0)
-    for step in range(1, hops - 1):
-        advance(0, step)
+    begin(0, 0)
     spread_done(1)
-    begin(1)
-    for step in range(hops - 1, hops + 1):
-        advance(0, step)
+    begin(0, 1)
+    advance_all(0, 1)
     spread_done(2)
-    attend(0, blk)
+    begin(1, 0)
+    advance_all(0, 2)
+    spread_done(3)
+    begin(1, 1)
+    for step in range(3, hops):
+        advance_all(0, step)
+    advance_all(1, 1)
+    advance_all(0, hops)
+    spread_done(4)
+    attend(0, [blk])
     for step in range(1, hops):
-        advance(1, step)
-        if step == hops - 1:
-            spread_done(3)
-            begin(2)
-        near(0, step)
-    advance(1, hops)
-    attend(0, lax.rem(blk + hops, nx))
-    spread_done(4)
-    attend(1, blk)
+        if step > 1:
+            advance_all(1, step)
+        attend(0, [behind(step), beyond(step)])
+        if step == 1:
+            spread_done(5)
+            begin(2, 0)
+        if step == 2:
+            spread_done(6)
+            begin(2, 1)
+    advance_all(1, hops)
+    advance_all(2, 1)
+    attend(0, [beyond(hops)])
+    spread_done(7)
+    attend(1, [blk])
     for step in range(1, hops):
-        advance(2, step)
-        near(1, step)
-    advance(2, hops)
-    attend(1, lax.rem(blk + hops, nx))
-
-    velocity = acc[0] / total[0] + acc[1] / total[1]
+        if step > 1:
+            advance_all(2, step)
+        attend(1, [behind(step), beyond(step)])
+    advance_all(2, hops)
+    attend(1, [beyond(hops)])
+
+    velocity = 0.0
+    for h in range(2):
+        velocity = velocity + acc[h, pl.ds(0, patch), :] / acc[h, pl.ds(patch, 1), :]
     velocity = velocity * jnp.where(cfg == 0, GUIDE, 1.0 - GUIDE)
     later = pltpu.roll(velocity, rows - few, 1)
     wide[...] = jnp.concatenate([velocity, later], axis=0).T
@@ -378,8 +410,8 @@
                 pltpu.make_async_copy(tiles, tiles, psent.at[c, 0]).wait()
                 pltpu.make_async_copy(psend, psend, psent.at[c, 1]).wait()
 
-    for i in range(5):
-        sent = whole[i].at[pl.ds(0, rows - tok), :]
+    for i, (_, whole, count) in enumerate(parcels):
+        sent = whole.at[pl.ds(0, (nz - 1) * count), :]
         pltpu.make_async_copy(sent, sent, zsend.at[i]).wait()
     for c in range(3):
         for step in range(1, hops + 1):
@@ -419,10 +451,9 @@
             pltpu.VMEM((nz, tok, 2 * patch), jnp.bfloat16),
             pltpu.VMEM((3, nx, rows, HDIM), jnp.bfloat16),
             pltpu.VMEM((2, rows, HDIM), jnp.bfloat16),
-            pltpu.VMEM((nx, 2 * patch, rows), jnp.bfloat16),
+            pltpu.VMEM((nx, 2, patch + ONES, rows), jnp.bfloat16),
             pltpu.VMEM((2, 1, rows), jnp.float32),
-            pltpu.VMEM((2, 1, rows), jnp.float32),
-            pltpu.VMEM((2, patch, rows), jnp.float32),
+            pltpu.VMEM((2, patch + ONES, rows), jnp.float32),
             pltpu.VMEM((rows, 2 * patch), jnp.float32),
             pltpu.VMEM((nz, tok // 2, 2 * patch), jnp.bfloat16),
             pltpu.VMEM((2 * nz, tok // 2, 2 * patch), jnp.bfloat16),
@@ -433,8 +464,8 @@
             pltpu.VMEM((pixels, 3 * TAP_LANES), jnp.float32),
             pltpu.VMEM((2, 3 * TAP_LANES, wide), jnp.bfloat16),
             pltpu.VMEM((8 * frames * COLS_DEV, wide), jnp.float32),
-            pltpu.SemaphoreType.DMA((5,)),
-            pltpu.SemaphoreType.DMA((5,)),
+            pltpu.SemaphoreType.DMA((8,)),
+            pltpu.SemaphoreType.DMA((8,)),
             pltpu.SemaphoreType.DMA((3, 2, nx // 2, 2)),
             pltpu.SemaphoreType.DMA((3, 2, nx // 2, 2)),
             pltpu.SemaphoreType.DMA,

time: 144 us -> 133 us (0.924)
  Pallas kernels: 141 us -> 130 us
    pallas_call x1, Pallas kernels: 141 us -> 130 us  [local(): pl.pallas_call(functools.partial(exchange_kernel, nz, nx), out_shape=jax....]
where the time goes in v3:
time: 133 us; the launch traced here: 132 us
  Pallas kernels  130 us (98%)
  local copies, waits for them, and re-layouts  2.79 us (2%)
    pallas_call x1, Pallas kernels, local(): pl.pallas_call(functools.partial(exchange_kernel, nz, nx), out_shape=jax....  130 us

profile of v3, /device:TPU:65, one launch (start us, length us, event | category | flops | bytes accessed | tf_op | source)
XLA Modules:
  0.0 132.5 jit_solution(3736912295786488539)
XLA Ops:
  0.0 0.0 copy-start
  0.0 0.7 copy-done
  0.7 0.6 reshape.19.bias_ref
  1.2 129.7 %shard_map.100 = bf16[4,6,4,384]{3,2,1,0:T(4,128)(2,1)} custom-call(bf16[48,4096]{1,0:T(8,128)(2,1)} %bitcast.10, bf16[48,4096]{1,0:T(8,128)(2,1)} %bitcast.11, bf16[48,4096]{1,0:T(8,128)(2,1)} %bitcast.12, bf16[64,4096]{1,0:T(8,128)(2,1)} %bitcast.9, f32[48,64]{1,0:T(8,128)} %noisy_ref.1, s32[1,48]{1,0:T(1,128)} %bitcast.15, f32[1,16]{1,0:T(1,128)} %bitcast.16, ...), custom_call_target="tpu_custom_call" | custom-call | tf_op jit(solution)/shard_map/pallas_call | solution.py:445
  131.0 1.5 %copy.12 = bf16[4,4,6,384]{3,1,2,0:T(4,128)(2,1)} copy(bf16[4,4,6,384]{3,1,2,0:T(4,128)(2,1)} %bitcast.14) | data formatting | bytes 147456
Async XLA Ops:
  0.0 0.7 copy-start
